TPU v7x, 64 devices: a 2x2x8 block of a 4x4x8 slice. The times are simulated.
64 devices in a mesh: rep: 4 (over x, y), dp: 16 (over z, core).
Axes of the slice: x: 2, y: 2, z: 8, core: 2. Of those that a mesh axis runs over, the one named last changes fastest.
The devices are a block of a 4x4x8 slice.
Arguments:
- g_w_gate: bfloat16 [64, 2, 1024, 2816], P(('rep', 'dp')), parts along dimension 0
- g_w_up: bfloat16 [64, 2, 1024, 2816], P(('rep', 'dp')), parts along dimension 0
- g_w_down: bfloat16 [64, 2, 2816, 1024], P(('rep', 'dp')), parts along dimension 0
- w_gate: bfloat16 [2, 1024, 2816], replicated
- w_up: bfloat16 [2, 1024, 2816], replicated
- w_down: bfloat16 [2, 2816, 1024], replicated
- m_w_gate: float32 [2, 1024, 2816], P(None, 'dp')
- m_w_up: float32 [2, 1024, 2816], P(None, 'dp')
- m_w_down: float32 [2, 2816, 1024], P(None, 'dp')
- v_w_gate: float32 [2, 1024, 2816], P(None, 'dp')
- v_w_up: float32 [2, 1024, 2816], P(None, 'dp')
- v_w_down: float32 [2, 2816, 1024], P(None, 'dp')
Outputs:
- output 1: bfloat16 [8, 1024, 2816], P('rep'), parts along dimension 0
- output 2: bfloat16 [8, 1024, 2816], P('rep'), parts along dimension 0
- output 3: bfloat16 [8, 2816, 1024], P('rep'), parts along dimension 0
- output 4: float32 [8, 1024, 2816], P('rep', 'dp'), parts along dimension 0
- output 5: float32 [8, 1024, 2816], P('rep', 'dp'), parts along dimension 0
- output 6: float32 [8, 2816, 1024], P('rep', 'dp'), parts along dimension 0
- output 7: float32 [8, 1024, 2816], P('rep', 'dp'), parts along dimension 0
- output 8: float32 [8, 1024, 2816], P('rep', 'dp'), parts along dimension 0
- output 9: float32 [8, 2816, 1024], P('rep', 'dp'), parts along dimension 0
There are 4 independent parts. A program takes and returns all parts, laid end to end along the dimension named above; an argument that names none is the same for every part.
All inputs are finite; a program needn't handle non-finite values.
Results may differ from a plain program's by a relative error of at most 0.022.
Values are sent between devices in bfloat16 or wider.
A program may use at most 768 MiB of HBM per device.

v0:
```python
import jax
import jax.numpy as jnp
from jax import lax
from jax.sharding import PartitionSpec as P


def adamw(w, m, v, g):
    m = 0.9 * m + 0.1 * g
    v = 0.95 * v + 0.05 * g * g
    step = m * lax.rsqrt(v + 1e-8) + 0.1 * w
    return (w - 0.02 * step).astype(jnp.bfloat16), m, v


def solution(mesh):
    def step(*arrays):
        terms, weights, m, v = (arrays[i : i + 3] for i in (0, 3, 6, 9))
        gradients = [lax.psum_scatter(t[0], "dp", scatter_dimension=1, tiled=True).astype(jnp.float32) for t in terms]
        me = lax.axis_index("dp")
        own = [lax.dynamic_slice_in_dim(w, me * one.shape[1], one.shape[1], 1).astype(jnp.float32) for w, one in zip(weights, m, strict=True)]
        new = [adamw(w, m, v, g) for w, m, v, g in zip(own, m, v, gradients, strict=True)]
        whole = [lax.all_gather(one[0], "dp", axis=1, tiled=True) for one in new]
        return (*whole, *(one[1] for one in new), *(one[2] for one in new))

    all_of, cut = P(None, None, None), P(None, "dp", None)
    return jax.shard_map(
        step,
        mesh=mesh,
        in_specs=(P(("rep", "dp"), None, None, None),) * 3 + (all_of,) * 3 + (cut,) * 6,
        out_specs=(P("rep", None, None),) * 3 + (P("rep", "dp", None),) * 6,
        check_vma=False,
    )
```

profile of v0, /device:TPU:21, one launch (start us, length us, event | category | flops | bytes accessed | tf_op | source)
XLA Modules:
  0.0 474.7 jit_solution(8129109184678931093)
XLA Ops:
  7.2 0.1 reduce-scatter.8.cloned.1.call-start
  7.3 0.7 reduce-scatter.8.cloned.1.call-update
  8.0 0.1 reduce-scatter.6.cloned.1.call-start
  8.1 0.7 reduce-scatter.6.cloned.1.call-update
  8.8 0.1 reduce-scatter.4.cloned.1.call-start
  8.9 0.0 copy-start.1
  8.9 0.0 copy-start.2
  8.9 0.7 reduce-scatter.4.cloned.1.call-update
  9.6 0.1 all-gather.8.cloned.1.call-start
  9.7 76.2 %reduce-scatter.8.cloned.1.call-done = bf16[2,176,1024]{2,1,0:T(8,128)(2,1)} async-done(((bf16[2,2816,1024]{2,1,0:T(8,128)(2,1)}), bf16[2,176,1024]{2,1,0:T(8,128)(2,1)}) %reduce-scatter.8.cloned.1.call-update) | async-done | bytes 720912 | tf_op jit(solution)/shard_map/reduce_scatter | solution.py:17
  85.9 0.0 copy-done.1
  85.9 0.0 copy-done.2
  85.9 3.6 fusion.10
  89.5 0.1 all-gather.8.cloned.1.call-update
  89.5 0.1 all-gather.6.cloned.1.call-start
  89.6 71.5 %reduce-scatter.6.cloned.1.call-done = bf16[2,64,2816]{2,1,0:T(8,128)(2,1)} async-done(((bf16[2,1024,2816]{2,1,0:T(8,128)(2,1)}), bf16[2,64,2816]{2,1,0:T(8,128)(2,1)}) %reduce-scatter.6.cloned.1.call-update) | async-done | bytes 720912 | tf_op jit(solution)/shard_map/reduce_scatter | solution.py:17
  161.0 4.5 fusion.6
  165.6 0.1 all-gather.6.cloned.1.call-update
  165.6 0.1 all-gather.4.cloned.1.call-start
  165.7 70.5 %reduce-scatter.4.cloned.1.call-done = bf16[2,64,2816]{2,1,0:T(8,128)(2,1)} async-done(((bf16[2,1024,2816]{2,1,0:T(8,128)(2,1)}), bf16[2,64,2816]{2,1,0:T(8,128)(2,1)}) %reduce-scatter.4.cloned.1.call-update) | async-done | bytes 720912 | tf_op jit(solution)/shard_map/reduce_scatter | solution.py:17
  236.2 0.0 copy-done.3
  236.2 0.0 copy-done.4
  236.2 3.5 fusion.2
  239.7 0.1 all-gather.4.cloned.1.call-update
  239.8 68.2 %all-gather.8.cloned.1.call-done = bf16[2,2816,1024]{2,1,0:T(8,128)(2,1)} async-done(((bf16[2,176,1024]{2,1,0:T(8,128)(2,1)}), bf16[2,2816,1024]{2,1,0:T(8,128)(2,1)}) %all-gather.8.cloned.1.call-update) | async-done | bytes 11534352 | tf_op jit(solution)/shard_map/all_gather | solution.py:21
  308.0 67.9 %all-gather.6.cloned.1.call-done = bf16[2,1024,2816]{2,1,0:T(8,128)(2,1)} async-done(((bf16[2,64,2816]{2,1,0:T(8,128)(2,1)}), bf16[2,1024,2816]{2,1,0:T(8,128)(2,1)}) %all-gather.6.cloned.1.call-update) | async-done | bytes 11534352 | tf_op jit(solution)/shard_map/all_gather | solution.py:21
  375.9 68.0 %all-gather.4.cloned.1.call-done = bf16[2,1024,2816]{2,1,0:T(8,128)(2,1)} async-done(((bf16[2,64,2816]{2,1,0:T(8,128)(2,1)}), bf16[2,1024,2816]{2,1,0:T(8,128)(2,1)}) %all-gather.4.cloned.1.call-update) | async-done | bytes 11534352 | tf_op jit(solution)/shard_map/all_gather | solution.py:21
  443.9 11.7 %copy.24 = bf16[2,1024,2816]{2,1,0:T(8,128)(2,1)} copy(bf16[2,1024,2816]{2,1,0:T(8,128)(2,1)} %all-gather.4.cloned.1.call-done) | data formatting | bytes 23068672
  455.6 5.8 %copy.25 = bf16[2,1024,2816]{2,1,0:T(8,128)(2,1)} copy(bf16[2,1024,2816]{2,1,0:T(8,128)(2,1)S(1)} %copy-done) | data formatting | bytes 23068672
  461.4 0.8 slice-done.1
  462.2 1.2 slice-done.2
  463.4 4.4 copy.26
  (9 shorter events, 0.0 us)
Async XLA Ops:
  7.2 78.7 %reduce-scatter.8.cloned.1.call-start = ((), (), s32[]{:S(2)}) async-start(), calls=%async_computation.7 | async-start | bytes 12255232 | tf_op jit(solution)/shard_map/reduce_scatter | solution.py:17
  8.0 153.1 %reduce-scatter.6.cloned.1.call-start = ((), (), s32[]{:S(2)}) async-start(), calls=%async_computation.5 | async-start | bytes 12255232 | tf_op jit(solution)/shard_map/reduce_scatter | solution.py:17
  8.8 227.4 %reduce-scatter.4.cloned.1.call-start = ((), (), s32[]{:S(2)}) async-start(), calls=%async_computation.3 | async-start | bytes 12255232 | tf_op jit(solution)/shard_map/reduce_scatter | solution.py:17
  8.9 77.0 %copy-start.1 = (f32[2,176,1024]{2,1,0:T(8,128)S(1)}, f32[2,176,1024]{2,1,0:T(8,128)}, u32[]{:S(2)}) copy-start(f32[2,176,1024]{2,1,0:T(8,128)} %param.23) | copy-start | bytes 4325380
  8.9 77.0 %copy-start.2 = (f32[2,176,1024]{2,1,0:T(8,128)S(1)}, f32[2,176,1024]{2,1,0:T(8,128)}, u32[]{:S(2)}) copy-start(f32[2,176,1024]{2,1,0:T(8,128)} %param.20) | copy-start | bytes 4325380
  9.6 298.4 %all-gather.8.cloned.1.call-start = ((), (), s32[]{:S(2)}) async-start(), calls=%async_computation.8 | async-start | bytes 12255232 | tf_op jit(solution)/shard_map/all_gather | solution.py:21
  89.5 286.4 %all-gather.6.cloned.1.call-start = ((), (), s32[]{:S(2)}) async-start(), calls=%async_computation.6 | async-start | bytes 12255232 | tf_op jit(solution)/shard_map/all_gather | solution.py:21
  161.0 75.2 %copy-start.3 = (f32[2,64,2816]{2,1,0:T(8,128)S(1)}, f32[2,64,2816]{2,1,0:T(8,128)}, u32[]{:S(2)}) copy-start(f32[2,64,2816]{2,1,0:T(8,128)} %param.21) | copy-start | bytes 4325380
  161.0 75.2 %copy-start.4 = (f32[2,64,2816]{2,1,0:T(8,128)S(1)}, f32[2,64,2816]{2,1,0:T(8,128)}, u32[]{:S(2)}) copy-start(f32[2,64,2816]{2,1,0:T(8,128)} %param.18) | copy-start | bytes 4325380
  165.6 278.2 %all-gather.4.cloned.1.call-start = ((), (), s32[]{:S(2)}) async-start(), calls=%async_computation.4 | async-start | bytes 12255232 | tf_op jit(solution)/shard_map/all_gather | solution.py:21
  443.9 11.7 %copy-start = (bf16[2,1024,2816]{2,1,0:T(8,128)(2,1)S(1)}, bf16[2,1024,2816]{2,1,0:T(8,128)(2,1)}, u32[]{:S(2)}) copy-start(bf16[2,1024,2816]{2,1,0:T(8,128)(2,1)} %all-gather.6.cloned.1.call-done) | copy-start | bytes 34603012
  443.9 17.5 %slice-start = ((s8[11534336]{0:T(1024)(128)(4,1)}), s8[4194304]{0:T(1024)(128)(4,1)S(1)}, s32[]{:S(2)}) async-start(s8[11534336]{0:T(1024)(128)(4,1)} %bitcast.6), calls=%async_computation.9 | async-start | bytes 8388608
  443.9 18.3 %slice-start.1 = ((s8[11534336]{0:T(1024)(128)(4,1)}), s8[4194304]{0:T(1024)(128)(4,1)S(1)}, s32[]{:S(2)}) async-start(s8[11534336]{0:T(1024)(128)(4,1)} %bitcast.6), calls=%async_computation.10 | async-start | bytes 8388608
  455.5 7.9 %slice-start.2 = ((s8[11534336]{0:T(1024)(128)(4,1)}), s8[3145728]{0:T(1024)(128)(4,1)S(1)}, s32[]{:S(2)}) async-start(s8[11534336]{0:T(1024)(128)(4,1)} %bitcast.6), calls=%async_computation.11 | async-start | bytes 6291456
Sparse Core Ops, SparseCore 0:
  10.4 75.4 reduce-scatter.7
  88.2 72.7 reduce-scatter.5
  163.4 72.7 reduce-scatter.3
  238.3 69.6 all-gather.7
  310.0 65.8 all-gather.5
  378.0 65.8 all-gather.3
where the time goes:
time: 475 us
  waiting for transfers between devices  425 us (89%)
  local copies, waits for them, and re-layouts  24 us (5%)
  between operations  14.2 us (3%)
  other arithmetic  11.6 us (2%)
    reduce_scatter x3, waiting for transfers between devices, step(): lax.psum_scatter(t[0], 'dp', scatter_dimension=1, tiled=True)  218 us
    all_gather x3, waiting for transfers between devices, step(): whole = [lax.all_gather(one[0], 'dp', axis=1, tiled=True) for one in new]  204 us
    unnamed x19, local copies, waits for them, and re-layouts  24 us
    convert_element_type x3, other arithmetic, adamw(): return ((w - 0.02 * step).astype(jnp.bfloat16), m, v)  11.6 us
  transfers between devices with their start and end apart: 6, of which 6 were waited for; matrix products, arithmetic and copies ran while one was open for 2% of the time, Pallas kernels for 0%

commit v1 on v0

v1 whole, which is shorter than its diff:
```python
import functools

import jax
import jax.numpy as jnp
from jax import lax
from jax.experimental import pallas as pl
from jax.experimental.pallas import tpu as pltpu
from jax.sharding import PartitionSpec as P

CORES = 2
ROWS = 16
WAYS = 2


def adamw(w, m, v, g):
    m = 0.9 * m + 0.1 * g
    v = 0.95 * v + 0.05 * g * g
    step = m * lax.rsqrt(v + 1e-8) + 0.1 * w
    return (w - 0.02 * step).astype(jnp.bfloat16), m, v


def kernel(chips, count, *refs):
    def take(number):
        nonlocal refs
        head, refs = refs[:number], refs[number:]
        return head

    g, w, m, v = (take(count) for _ in range(4))
    w_out, m_out, v_out = (take(count) for _ in range(3))
    given, came, own, wb, mb, vb = (take(count) for _ in range(6))
    own_sem, give_send, give_recv, ring_send, ring_recv, in_sem, out_sem, ag_send, ag_recv, side_send, side_recv = refs

    me = lax.axis_index("dp")
    z, c = me // CORES, me % CORES
    other = 1 - c

    def chip(i):
        return (i + 2 * chips) % chips

    partner = {"dp": z * CORES + other}
    ahead = [{"dp": chip(z + 1) * CORES + c}, {"dp": chip(z - 1) * CORES + c}]
    parts = [(k, d) for k in range(count) for d in range(WAYS)]
    half = [one.shape[0] // WAYS for one in m]
    rows = [one.shape[1] for one in m]

    def block(k, d, chip_of, core):
        start = pl.multiple_of((chip_of * CORES + core) * rows[k], rows[k])
        return pl.ds(d * half[k], half[k]), pl.ds(start, rows[k])

    def turn(d, s):
        return chip(z - 1 - s) if d == 0 else chip(z + 1 + s)

    def load_own(s, k, d):
        layers, where = block(k, d, turn(d, s), c)
        return pltpu.make_async_copy(g[k].at[0, layers, where], own[k].at[s % 2, d], own_sem.at[s % 2, k, d])

    def give(s, k, d):
        layers, where = block(k, d, turn(d, s), other)
        return pltpu.make_async_remote_copy(
            g[k].at[0, layers, where], given[k].at[s, d], give_send.at[s, k, d], give_recv.at[s, k, d], device_id=partner
        )

    def ring(s, k, d):
        return pltpu.make_async_remote_copy(
            given[k].at[s, d], came[k].at[s, d], ring_send.at[s, k, d], ring_recv.at[s, k, d], device_id=ahead[d]
        )

    def load_state(k, d):
        layers, where = block(k, d, z, c)
        return [
            pltpu.make_async_copy(w[k].at[layers, where], wb[k].at[d], in_sem.at[0, k, d]),
            pltpu.make_async_copy(m[k].at[layers], mb[k].at[d], in_sem.at[1, k, d]),
            pltpu.make_async_copy(v[k].at[layers], vb[k].at[d], in_sem.at[2, k, d]),
        ]

    def store_state(k, d):
        layers, where = block(k, d, z, c)
        return [
            pltpu.make_async_copy(wb[k].at[d], w_out[k].at[layers, where], out_sem.at[0, k, d]),
            pltpu.make_async_copy(mb[k].at[d], m_out[k].at[layers], out_sem.at[1, k, d]),
            pltpu.make_async_copy(vb[k].at[d], v_out[k].at[layers], out_sem.at[2, k, d]),
        ]

    def gathered(t, k, d):
        layers, where = block(k, d, chip(z - t) if d == 0 else chip(z + t), c)
        return w_out[k].at[layers, where]

    def gather(t, k, d):
        here = gathered(t, k, d)
        return pltpu.make_async_remote_copy(
            wb[k].at[d] if isinstance(t, int) and t == 0 else here, here, ag_send.at[t, k, d], ag_recv.at[t, k, d], device_id=ahead[d]
        )

    def gather_recv(t, k, d):
        here = gathered(t + 1, k, d)
        return pltpu.make_async_remote_copy(here, here, ag_send.at[t, k, d], ag_recv.at[t, k, d], device_id=ahead[d])

    def side(t, k, d):
        here = gathered(t, k, d)
        return pltpu.make_async_remote_copy(
            wb[k].at[d] if isinstance(t, int) and t == 0 else here, here, side_send.at[t, k, d], side_recv.at[t, k, d], device_id=partner
        )

    def side_recv_of(t, k, d):
        layers, where = block(k, d, chip(z - t) if d == 0 else chip(z + t), other)
        here = w_out[k].at[layers, where]
        return pltpu.make_async_remote_copy(here, here, side_send.at[t, k, d], side_recv.at[t, k, d], device_id=partner)

    def by_rows(k, body):
        for h in range(half[k]):

            @pl.loop(0, rows[k] // ROWS)
            def _(i):
                body(h, pl.ds(pl.multiple_of(i * ROWS, ROWS), ROWS))

    def total(s, k, d, h, at, first):
        so_far = own[k][s % 2, d, h, at].astype(jnp.float32) + given[k][s, d, h, at].astype(jnp.float32)
        if not first:
            so_far = so_far + came[k][s - 1, d, h, at].astype(jnp.float32)
        return so_far.astype(jnp.bfloat16)

    def arrive(s, k, d, first):
        load_own(s, k, d).wait()
        give(s, k, d).wait_recv()
        if not first:
            ring(s - 1, k, d).wait_recv()

    def add(s, k, d, first):
        arrive(s, k, d, first)

        def body(h, at):
            given[k][s, d, h, at] = total(s, k, d, h, at, first)

        by_rows(k, body)
        ring(s, k, d).start()

    def update(s, k, d):
        arrive(s, k, d, False)
        for copy in load_state(k, d):
            copy.wait()

        def body(h, at):
            grad = total(s, k, d, h, at, False).astype(jnp.float32)
            one = adamw(wb[k][d, h, at].astype(jnp.float32), mb[k][d, h, at], vb[k][d, h, at], grad)
            wb[k][d, h, at], mb[k][d, h, at], vb[k][d, h, at] = one

        by_rows(k, body)
        gather(0, k, d).start()
        side(0, k, d).start()
        for copy in store_state(k, d):
            copy.start()

    barrier = pltpu.get_barrier_semaphore()
    for device in (*ahead, partner):
        pl.semaphore_signal(barrier, inc=1, device_id=device)
    for k, d in parts:
        load_own(0, k, d).start()
    pl.semaphore_wait(barrier, 3)
    for k, d in parts:
        give(0, k, d).start()
    for k, d in parts:
        load_own(1, k, d).start()
        give(1, k, d).start()

    def onward(s, k, d):
        load_own(s + 2, k, d).start()
        give(s + 2, k, d).start()

    last = chips - 1
    for k, d in parts:
        add(0, k, d, True)
        onward(0, k, d)
    for k, d in parts:
        for copy in load_state(k, d):
            copy.start()

    @pl.loop(1, last - 1)
    def _(s):
        for k, d in parts:
            add(s, k, d, False)
            onward(s, k, d)

    for k, d in parts:
        add(last - 1, k, d, False)
    for k, d in parts:
        update(last, k, d)

    @pl.loop(1, last)
    def _(t):
        for k, d in parts:
            gather_recv(t - 1, k, d).wait_recv()
            gather(t, k, d).start()
            side(t, k, d).start()

    for k, d in parts:
        gather_recv(last - 1, k, d).wait_recv()
        side(last, k, d).start()

    for k, d in parts:
        for copy in store_state(k, d):
            copy.wait()
        gather(0, k, d).wait_send()
        side(0, k, d).wait_send()

    @pl.loop(0, last)
    def _(s):
        for k, d in parts:
            give(s, k, d).wait_send()
            ring(s, k, d).wait_send()
            side_recv_of(s, k, d).wait_recv()

    @pl.loop(1, last)
    def _(t):
        for k, d in parts:
            gather(t, k, d).wait_send()
            side(t, k, d).wait_send()

    for k, d in parts:
        give(last, k, d).wait_send()
        side(last, k, d).wait_send()
        side_recv_of(last, k, d).wait_recv()


def solution(mesh):
    chips = mesh.shape["dp"] // CORES

    def step(*arrays):
        terms, weights, m, v = (arrays[i : i + 3] for i in (0, 3, 6, 9))
        count = len(weights)
        shapes = [(one.shape[0] // WAYS, *one.shape[1:]) for one in m]
        any_of = pl.BlockSpec(memory_space=pl.ANY)
        dma = pltpu.SemaphoreType.DMA
        out = pl.pallas_call(
            functools.partial(kernel, chips, count),
            out_shape=[jax.ShapeDtypeStruct(one.shape, one.dtype) for one in (*weights, *m, *v)],
            in_specs=[any_of] * len(arrays),
            out_specs=[any_of] * (3 * count),
            scratch_shapes=[
                *(pltpu.VMEM((chips, WAYS, *one), jnp.bfloat16) for one in shapes),
                *(pltpu.VMEM((chips - 1, WAYS, *one), jnp.bfloat16) for one in shapes),
                *(pltpu.VMEM((2, WAYS, *one), jnp.bfloat16) for one in shapes),
                *(pltpu.VMEM((WAYS, *one), jnp.bfloat16) for one in shapes),
                *(pltpu.VMEM((WAYS, *one), jnp.float32) for one in shapes),
                *(pltpu.VMEM((WAYS, *one), jnp.float32) for one in shapes),
                dma((2, count, WAYS)),
                dma((chips, count, WAYS)),
                dma((chips, count, WAYS)),
                dma((chips - 1, count, WAYS)),
                dma((chips - 1, count, WAYS)),
                dma((3, count, WAYS)),
                dma((3, count, WAYS)),
                dma((chips - 1, count, WAYS)),
                dma((chips - 1, count, WAYS)),
                dma((chips, count, WAYS)),
                dma((chips, count, WAYS)),
            ],
            compiler_params=pltpu.CompilerParams(collective_id=0, has_side_effects=True, vmem_limit_bytes=60 * 1024 * 1024),
        )(*terms, *weights, *m, *v)
        return tuple(out)

    all_of, cut = P(None, None, None), P(None, "dp", None)
    return jax.shard_map(
        step,
        mesh=mesh,
        in_specs=(P(("rep", "dp"), None, None, None),) * 3 + (all_of,) * 3 + (cut,) * 6,
        out_specs=(P("rep", None, None),) * 3 + (P("rep", "dp", None),) * 6,
        check_vma=False,
    )
```

time: 475 us -> 377 us (0.79)
  waiting for transfers between devices: 425 us -> 0 us
  Pallas kernels: 0 us -> 342 us
  between operations: 14.2 us -> 0.69 us
  other arithmetic: 11.6 us -> 0.01 us
  local copies, waits for them, and re-layouts: 24 us -> 34.5 us
    pallas_call x0 -> x1, Pallas kernels: none -> 342 us  [step(): pl.pallas_call(functools.partial(kernel, chips, count), out_shape=[jax.Sh...]
    reduce_scatter x3 -> x0, waiting for transfers between devices: 218 us -> none  [step(): lax.psum_scatter(t[0], 'dp', scatter_dimension=1, tiled=True)]
    all_gather x3 -> x0, waiting for transfers between devices: 204 us -> none  [step(): whole = [lax.all_gather(one[0], 'dp', axis=1, tiled=True) for one in new]]
    convert_element_type x3 -> x0, other arithmetic: 11.6 us -> none  [adamw(): return ((w - 0.02 * step).astype(jnp.bfloat16), m, v)]
    unnamed x19 -> x29, local copies, waits for them, and re-layouts: 24 us -> 34.5 us
  transfers between devices with their start and end apart: 6 -> 0, of which waited for: 6 -> 0; matrix products, arithmetic and copies ran while one was open for 2% -> 0% of each run, Pallas kernels for 0% -> 0%
where the time goes in v1:
time: 377 us
  Pallas kernels  342 us (91%)
  local copies, waits for them, and re-layouts  34.5 us (9%)
    pallas_call x1, Pallas kernels, step(): pl.pallas_call(functools.partial(kernel, chips, count), out_shape=[jax.Sh...  342 us
    unnamed x29, local copies, waits for them, and re-layouts  34.5 us

profile of v1, /device:TPU:21, one launch (start us, length us, event | category | flops | bytes accessed | tf_op | source)
XLA Modules:
  0.0 376.9 jit_solution(9739882661532971172)
XLA Ops:
  0.6 341.8 %shard_map.187 = (bf16[2,1024,2816]{2,1,0:T(8,128)(2,1)}, bf16[2,1024,2816]{2,1,0:T(8,128)(2,1)}, bf16[2,2816,1024]{2,1,0:T(8,128)(2,1)}, f32[2,64,2816]{2,1,0:T...) custom-call(bf16[1,2,1024,2816]{3,2,1,0:T(8,128)(2,1)} %refs_0_.1, ...), custom_call_target="tpu_custom_call" | custom-call | tf_op jit(solution)/shard_map/pallas_call | solution.py:233
  342.4 0.0 copy-start
  342.4 0.0 slice-start
  342.4 0.0 slice-start.1
  342.5 11.7 %copy.30 = bf16[2,1024,2816]{2,1,0:T(8,128)(2,1)} copy(bf16[2,1024,2816]{2,1,0:T(8,128)(2,1)} %get-tuple-element.18) | data formatting | bytes 23068672
  354.1 0.0 copy-done
  354.1 0.0 slice-start.2
  354.1 5.8 %copy.31 = bf16[2,1024,2816]{2,1,0:T(8,128)(2,1)} copy(bf16[2,1024,2816]{2,1,0:T(8,128)(2,1)S(1)} %copy-done) | data formatting | bytes 23068672
  360.0 0.0 slice-done
  360.0 0.7 slice-done.1
  360.7 1.3 slice-done.2
  362.0 0.0 copy-start.6
  362.0 4.4 %copy.32 = bf16[2,2816,1024]{2,1,0:T(8,128)(2,1)} copy(bf16[2,2816,1024]{2,1,0:T(8,128)(2,1)S(1)} %bitcast.1) | data formatting | bytes 23068672
  366.4 0.0 copy-done.6
  366.4 0.0 copy-start.5
  366.4 1.1 copy.33
  367.5 0.8 copy-done.5
  368.3 0.0 copy-start.4
  368.3 1.1 copy.34
  369.4 0.8 copy-done.4
  370.2 0.0 copy-start.3
  370.2 1.1 copy.35
  371.3 0.8 copy-done.3
  372.1 0.0 copy-start.2
  372.1 1.1 copy.36
  373.2 0.8 copy-done.2
  374.0 0.0 copy-start.1
  374.0 1.1 copy.37
  375.1 0.8 copy-done.1
  375.8 1.1 copy.38
  (1 shorter events, 0.0 us)
Async XLA Ops:
  342.4 11.7 %copy-start = (bf16[2,1024,2816]{2,1,0:T(8,128)(2,1)S(1)}, bf16[2,1024,2816]{2,1,0:T(8,128)(2,1)}, u32[]{:S(2)}) copy-start(bf16[2,1024,2816]{2,1,0:T(8,128)(2,1)} %get-tuple-element.19) | copy-start | bytes 34603012
  342.4 17.6 %slice-start = ((s8[11534336]{0:T(1024)(128)(4,1)}), s8[4194304]{0:T(1024)(128)(4,1)S(1)}, s32[]{:S(2)}) async-start(s8[11534336]{0:T(1024)(128)(4,1)} %bitcast), calls=%async_computation | async-start | bytes 8388608
  342.4 18.2 %slice-start.1 = ((s8[11534336]{0:T(1024)(128)(4,1)}), s8[4194304]{0:T(1024)(128)(4,1)S(1)}, s32[]{:S(2)}) async-start(s8[11534336]{0:T(1024)(128)(4,1)} %bitcast), calls=%async_computation.1 | async-start | bytes 8388608
  354.1 7.8 %slice-start.2 = ((s8[11534336]{0:T(1024)(128)(4,1)}), s8[3145728]{0:T(1024)(128)(4,1)S(1)}, s32[]{:S(2)}) async-start(s8[11534336]{0:T(1024)(128)(4,1)} %bitcast), calls=%async_computation.2 | async-start | bytes 6291456
  362.0 4.4 %copy-start.6 = (f32[2,64,2816]{2,1,0:T(8,128)S(1)}, f32[2,64,2816]{2,1,0:T(8,128)}, u32[]{:S(2)}) copy-start(f32[2,64,2816]{2,1,0:T(8,128)} %get-tuple-element.21) | copy-start | bytes 4325380
  366.4 1.9 copy-start.5
  368.3 1.9 copy-start.4
  370.2 1.9 copy-start.3
  372.1 1.9 copy-start.2
  374.0 1.9 copy-start.1

commit v2 on v1

v2 whole, which is shorter than its diff:
```python
import functools

import jax
import jax.numpy as jnp
from jax import lax
from jax.experimental import pallas as pl
from jax.experimental.pallas import tpu as pltpu
from jax.sharding import PartitionSpec as P

CORES = 2
ROWS = 16
WAYS = 2


def adamw(w, m, v, g):
    m = 0.9 * m + 0.1 * g
    v = 0.95 * v + 0.05 * g * g
    step = m * lax.rsqrt(v + 1e-8) + 0.1 * w
    return (w - 0.02 * step).astype(jnp.bfloat16), m, v


def kernel(chips, count, *refs):
    def take(number):
        nonlocal refs
        head, refs = refs[:number], refs[number:]
        return head

    g, w, m, v = (take(count) for _ in range(4))
    w_out, m_out, v_out = (take(count) for _ in range(3))
    own, wb = (take(count) for _ in range(2))
    own_sem, give_send, give_recv, ring_send, ring_recv, in_sem, ag_send, ag_recv, side_send, side_recv, free, clear = refs

    me = lax.axis_index("dp")
    z, c = me // CORES, me % CORES
    other = 1 - c

    def chip(i):
        return (i + 2 * chips) % chips

    partner = {"dp": z * CORES + other}
    ahead = [{"dp": chip(z + 1) * CORES + c}, {"dp": chip(z - 1) * CORES + c}]
    behind = ahead[::-1]
    parts = [(k, d) for k in range(count) for d in range(WAYS)]
    half = [one.shape[0] // WAYS for one in m]
    rows = [one.shape[1] for one in m]
    last = chips - 1

    def block(k, d, chip_of, core):
        start = pl.multiple_of((chip_of * CORES + core) * rows[k], rows[k])
        return pl.ds(d * half[k], half[k]), pl.ds(start, rows[k])

    def turn(d, s):
        return chip(z - 1 - s) if d == 0 else chip(z + 1 + s)

    def load_own(s, k, d):
        layers, where = block(k, d, turn(d, s), c)
        return pltpu.make_async_copy(g[k].at[0, layers, where], own[k].at[s % 2, d], own_sem.at[s % 2, k, d])

    def give(s, k, d):
        layers, where = block(k, d, turn(d, s), other)
        return pltpu.make_async_remote_copy(
            g[k].at[0, layers, where], w_out[k].at[layers, where], give_send.at[s, k, d], give_recv.at[s, k, d], device_id=partner
        )

    def ring(s, k, d):
        layers, where = block(k, d, turn(d, s), c)
        _, there = block(k, d, turn(d, s), other)
        return pltpu.make_async_remote_copy(
            w_out[k].at[layers, where], w_out[k].at[layers, there], ring_send.at[s, k, d], ring_recv.at[s, k, d], device_id=ahead[d]
        )

    def load_state(k, d):
        layers, where = block(k, d, z, c)
        return [
            pltpu.make_async_copy(w[k].at[layers, where], wb[k].at[d], in_sem.at[0, k, d]),
            pltpu.make_async_copy(m[k].at[layers], m_out[k].at[layers], in_sem.at[1, k, d]),
            pltpu.make_async_copy(v[k].at[layers], v_out[k].at[layers], in_sem.at[2, k, d]),
        ]

    def gathered(t, k, d):
        layers, where = block(k, d, chip(z - t) if d == 0 else chip(z + t), c)
        return w_out[k].at[layers, where]

    def gather(t, k, d):
        here = gathered(t, k, d)
        return pltpu.make_async_remote_copy(here, here, ag_send.at[t, k, d], ag_recv.at[t, k, d], device_id=ahead[d])

    def side(t, k, d):
        here = gathered(t, k, d)
        return pltpu.make_async_remote_copy(here, here, side_send.at[t, k, d], side_recv.at[t, k, d], device_id=partner)

    def by_rows(k, body):
        for h in range(half[k]):

            @pl.loop(0, rows[k] // ROWS)
            def _(i):
                body(h, i * ROWS)

    def at(k, d, chip_of, core, h, row):
        start = pl.multiple_of((chip_of * CORES + core) * rows[k] + row, ROWS)
        return d * half[k] + h, pl.ds(start, ROWS)

    def total(s, k, d, h, row, first):
        mine = own[k][s % 2, d, h, pl.ds(pl.multiple_of(row, ROWS), ROWS)]
        so_far = mine.astype(jnp.float32) + w_out[k][at(k, d, turn(d, s), c, h, row)].astype(jnp.float32)
        if not first:
            so_far = so_far + w_out[k][at(k, d, turn(d, s), other, h, row)].astype(jnp.float32)
        return so_far.astype(jnp.bfloat16)

    def arrive(s, k, d, first):
        load_own(s, k, d).wait()
        give(s, k, d).wait_recv()
        if not first:
            ring(s - 1, k, d).wait_recv()

    def add(s, k, d, first):
        arrive(s, k, d, first)

        def body(h, row):
            w_out[k][at(k, d, turn(d, s), c, h, row)] = total(s, k, d, h, row, first)

        by_rows(k, body)
        ring(s, k, d).start()
        if not first:
            ring(s - 1, k, d).wait_send()

    def update(k, d):
        arrive(last, k, d, False)
        for copy in load_state(k, d):
            copy.wait()

        def body(h, row):
            grad = total(last, k, d, h, row, False).astype(jnp.float32)
            here = pl.ds(pl.multiple_of(row, ROWS), ROWS)
            state = d * half[k] + h, here
            old = wb[k][d, h, here].astype(jnp.float32)
            new = adamw(old, m_out[k][state], v_out[k][state], grad)
            w_out[k][at(k, d, z, c, h, row)], m_out[k][state], v_out[k][state] = new

        by_rows(k, body)
        pl.semaphore_wait(clear.at[0, k, d], 1)
        gather(0, k, d).start()
        pl.semaphore_signal(free.at[k, d], inc=1, device_id=partner)

    def onward(s, k, d):
        load_own(s + 2, k, d).start()
        give(s + 2, k, d).start()

    barrier = pltpu.get_barrier_semaphore()
    for device in (*ahead, partner):
        pl.semaphore_signal(barrier, inc=1, device_id=device)
    for k, d in parts:
        load_own(0, k, d).start()
    pl.semaphore_wait(barrier, 3)
    for k, d in parts:
        give(0, k, d).start()
    for k, d in parts:
        load_own(1, k, d).start()
        give(1, k, d).start()

    for k, d in parts:
        add(0, k, d, True)
        onward(0, k, d)
    for k, d in parts:
        for copy in load_state(k, d):
            copy.start()

    @pl.loop(1, last - 1)
    def _(s):
        for k, d in parts:
            add(s, k, d, False)
            onward(s, k, d)

    for k, d in parts:
        add(last - 1, k, d, False)
        pl.semaphore_signal(clear.at[0, k, d], inc=1, device_id=behind[d])
    for i, (k, d) in enumerate(parts):
        update(k, d)
        if i:
            pl.semaphore_wait(free.at[*parts[i - 1]], 1)
            side(0, *parts[i - 1]).start()
    pl.semaphore_wait(free.at[*parts[-1]], 1)
    side(0, *parts[-1]).start()
    for k, d in parts:
        ring(last - 1, k, d).wait_send()
        pl.semaphore_signal(clear.at[1, k, d], inc=1, device_id=behind[d])

    @pl.loop(1, last - 1)
    def _(t):
        for k, d in parts:
            gather(t - 1, k, d).wait_recv()
            gather(t, k, d).start()
            side(t, k, d).start()

    for k, d in parts:
        gather(last - 2, k, d).wait_recv()
        pl.semaphore_wait(clear.at[1, k, d], 1)
        gather(last - 1, k, d).start()
        side(last - 1, k, d).start()
    for k, d in parts:
        gather(last - 1, k, d).wait_recv()
        side(last, k, d).start()

    @pl.loop(0, last)
    def _(s):
        for k, d in parts:
            give(s, k, d).wait_send()
            gather(s, k, d).wait_send()
            side(s, k, d).wait_send()
            side(s, k, d).wait_recv()

    for k, d in parts:
        give(last, k, d).wait_send()
        side(last, k, d).wait_send()
        side(last, k, d).wait_recv()


def settle(count, *refs):
    sources, targets, sem = refs[:count], refs[count : 2 * count], refs[-1]
    copies = [
        pltpu.make_async_copy(source.at[layer], target.at[layer], sem.at[i, layer])
        for i, (source, target) in enumerate(zip(sources, targets))
        for layer in range(source.shape[0])
    ]
    for copy in copies:
        copy.start()
    for copy in copies:
        copy.wait()


def solution(mesh):
    chips = mesh.shape["dp"] // CORES

    def step(*arrays):
        terms, weights, m, v = (arrays[i : i + 3] for i in (0, 3, 6, 9))
        count = len(weights)
        shapes = [(one.shape[0] // WAYS, *one.shape[1:]) for one in m]
        any_of, vmem = (pl.BlockSpec(memory_space=space) for space in (pl.ANY, pltpu.VMEM))
        dma = pltpu.SemaphoreType.DMA
        out = pl.pallas_call(
            functools.partial(kernel, chips, count),
            out_shape=[pltpu.VMEM(one.shape, one.dtype) for one in (*weights, *m, *v)],
            in_specs=[any_of] * len(arrays),
            out_specs=[vmem] * (3 * count),
            scratch_shapes=[
                *(pltpu.VMEM((2, WAYS, *one), jnp.bfloat16) for one in shapes),
                *(pltpu.VMEM((WAYS, *one), jnp.bfloat16) for one in shapes),
                dma((2, count, WAYS)),
                dma((chips, count, WAYS)),
                dma((chips, count, WAYS)),
                dma((chips - 1, count, WAYS)),
                dma((chips - 1, count, WAYS)),
                dma((3, count, WAYS)),
                dma((chips - 1, count, WAYS)),
                dma((chips - 1, count, WAYS)),
                dma((chips, count, WAYS)),
                dma((chips, count, WAYS)),
                pltpu.SemaphoreType.REGULAR((count, WAYS)),
                pltpu.SemaphoreType.REGULAR((2, count, WAYS)),
            ],
            compiler_params=pltpu.CompilerParams(collective_id=0, has_side_effects=True, vmem_limit_bytes=8 * 1024 * 1024),
        )(*(pltpu.with_memory_space_constraint(one, pltpu.HBM) for one in arrays))
        layers = max(one.shape[0] for one in weights)
        return pl.pallas_call(
            functools.partial(settle, len(out)),
            out_shape=[jax.ShapeDtypeStruct(one.shape, one.dtype) for one in out],
            in_specs=[vmem] * len(out),
            out_specs=[any_of] * len(out),
            scratch_shapes=[dma((len(out), layers))],
            compiler_params=pltpu.CompilerParams(vmem_limit_bytes=2 * 1024 * 1024),
        )(*(pltpu.with_memory_space_constraint(one, pltpu.VMEM) for one in out))

    all_of, cut = P(None, None, None), P(None, "dp", None)
    return jax.shard_map(
        step,
        mesh=mesh,
        in_specs=(P(("rep", "dp"), None, None, None),) * 3 + (all_of,) * 3 + (cut,) * 6,
        out_specs=(P("rep", None, None),) * 3 + (P("rep", "dp", None),) * 6,
        check_vma=False,
    )
```

time: 377 us -> 357 us (0.947)
  local copies, waits for them, and re-layouts: 34.5 us -> 0 us
  Pallas kernels: 342 us -> 356 us
    unnamed x29 -> x0, local copies, waits for them, and re-layouts: 34.5 us -> none
    pallas_call x1 -> x2, Pallas kernels: 342 us -> 356 us  [the longest x1 342 us: step(): pl.pallas_call(functools.partial(kernel, chips, count), out_shape=[pltpu....]
where the time goes in v2:
time: 357 us; the launch traced here: 356 us
  Pallas kernels  356 us (100%)
    pallas_call x1, Pallas kernels, step(): pl.pallas_call(functools.partial(kernel, chips, count), out_shape=[pltpu....  342 us
    pallas_call x1, Pallas kernels, step(): pl.pallas_call(functools.partial(settle, len(out)), out_shape=[jax.ShapeD...  14 us

profile of v2, /device:TPU:21, one launch (start us, length us, event | category | flops | bytes accessed | tf_op | source)
XLA Modules:
  0.0 356.5 jit_solution(7765181557238948041)
XLA Ops:
  0.6 341.8 %shard_map.187 = (bf16[2,1024,2816]{2,1,0:T(8,128)(2,1)S(1)}, bf16[2,1024,2816]{2,1,0:T(8,128)(2,1)S(1)}, bf16[2,2816,1024]{2,1,0:T(8,128)(2,1)S(1)}, f32[2,64,2...) custom-call(bf16[1,2,1024,2816]{3,2,1,0:T(8,128)(2,1)} %refs_0_.1, ...), custom_call_target="tpu_custom_call" | custom-call | tf_op jit(solution)/shard_map/pallas_call | solution.py:240
  342.5 14.0 %shard_map.188 = (bf16[2,1024,2816]{2,1,0:T(8,128)(2,1)}, bf16[2,1024,2816]{2,1,0:T(8,128)(2,1)}, bf16[2,2816,1024]{2,1,0:T(8,128)(2,1)}, f32[2,64,2816]{2,1,0:T...) custom-call(bf16[2,1024,2816]{2,1,0:T(8,128)(2,1)S(1)} %get-tuple-el, ...), custom_call_target="tpu_custom_call" | custom-call | tf_op jit(solution)/shard_map/pallas_call | solution.py:264

commit v3 on v0

v3 whole, which is shorter than its diff:
```python
import functools
import types

import jax
import jax.numpy as jnp
from jax import lax
from jax.experimental import pallas as pl
from jax.experimental.pallas import tpu as pltpu
from jax.sharding import PartitionSpec as P

CORES = 2
ROWS = 16
WAYS = 2
LATE = 1
PIECES = 4


def adamw(w, m, v, g):
    m = 0.9 * m + 0.1 * g
    v = 0.95 * v + 0.05 * g * g
    step = m * lax.rsqrt(v + 1e-8) + 0.1 * w
    return (w - 0.02 * step).astype(jnp.bfloat16), m, v


def cut(rows, pieces):
    tiles = rows // ROWS
    ends = [tiles * i // pieces * ROWS for i in range(pieces + 1)]
    return [(a, b - a) for a, b in zip(ends, ends[1:]) if b > a]


def parts_of(state, pieces):
    return [(k, d, *piece) for k, one in enumerate(state) for piece in cut(one.shape[-2], pieces) for d in range(WAYS)]


def place(chips):
    me = lax.axis_index("dp")
    z, c = me // CORES, me % CORES

    def chip(i):
        return (i + 2 * chips) % chips

    ahead = [{"dp": chip(z + 1) * CORES + c}, {"dp": chip(z - 1) * CORES + c}]
    return types.SimpleNamespace(
        chips=chips,
        last=chips - 1,
        z=z,
        c=c,
        other=1 - c,
        chip=chip,
        partner={"dp": z * CORES + 1 - c},
        ahead=ahead,
        behind=ahead[::-1],
        turn=lambda d, s: chip(z - 1 - s) if d == 0 else chip(z + 1 + s),
    )


def engine(at, parts, g, w_out, m_out, v_out, own, wb, sems, held=None):
    e = types.SimpleNamespace(parts=range(len(parts)))
    half = [one.shape[0] // WAYS for one in m_out]
    block_rows = [one.shape[1] for one in m_out]

    def layers(p):
        k, d, _, _ = parts[p]
        return pl.ds(d * half[k], half[k])

    def within(p):
        return pl.ds(parts[p][2], parts[p][3])

    def rows_of(p, chip_of, core):
        k, _, start, size = parts[p]
        return pl.ds(pl.multiple_of((chip_of * CORES + core) * block_rows[k] + start, ROWS), size)

    def slot(p, chip_of, core):
        return w_out[parts[p][0]].at[layers(p), rows_of(p, chip_of, core)]

    def load_own(s, p):
        k, d, _, _ = parts[p]
        here = g[k].at[0, layers(p), rows_of(p, at.turn(d, s), at.c)]
        return pltpu.make_async_copy(here, own[k].at[s % 2, d, :, within(p)], sems.own.at[s % 2, p])

    def give(s, p):
        k, d, _, _ = parts[p]
        if held is not None:
            kept = held[k].at[s, d, :, within(p)]
            return pltpu.make_async_copy(kept, slot(p, at.turn(d, s), at.c), sems.give_recv.at[s, p])
        where = rows_of(p, at.turn(d, s), at.other)
        return pltpu.make_async_remote_copy(
            g[k].at[0, layers(p), where],
            w_out[k].at[layers(p), where],
            sems.give_send.at[s, p],
            sems.give_recv.at[s, p],
            device_id=at.partner,
        )

    def ring(s, p):
        d = parts[p][1]
        return pltpu.make_async_remote_copy(
            slot(p, at.turn(d, s), at.c),
            slot(p, at.turn(d, s), at.other),
            sems.ring_send.at[s, p],
            sems.ring_recv.at[s, p],
            device_id=at.ahead[d],
        )

    def travelling(t, p):
        return slot(p, at.chip(at.z - t) if parts[p][1] == 0 else at.chip(at.z + t), at.c)

    def gather(t, p):
        here = travelling(t, p)
        return pltpu.make_async_remote_copy(
            here, here, sems.ag_send.at[t, p], sems.ag_recv.at[t, p], device_id=at.ahead[parts[p][1]]
        )

    def side(t, p):
        here = travelling(t, p)
        return pltpu.make_async_remote_copy(here, here, sems.side_send.at[t, p], sems.side_recv.at[t, p], device_id=at.partner)

    def by_rows(p, body):
        for h in range(half[parts[p][0]]):

            @pl.loop(0, parts[p][3] // ROWS)
            def _(i):
                body(h, i * ROWS)

    def tile(p, chip_of, core, h, row):
        k, d, start, _ = parts[p]
        first = pl.multiple_of((chip_of * CORES + core) * block_rows[k] + start + row, ROWS)
        return d * half[k] + h, pl.ds(first, ROWS)

    def total(s, p, h, row, first):
        k, d, start, _ = parts[p]
        mine = own[k][s % 2, d, h, pl.ds(pl.multiple_of(start + row, ROWS), ROWS)]
        so_far = mine.astype(jnp.float32) + w_out[k][tile(p, at.turn(d, s), at.c, h, row)].astype(jnp.float32)
        if not first:
            so_far = so_far + w_out[k][tile(p, at.turn(d, s), at.other, h, row)].astype(jnp.float32)
        return so_far.astype(jnp.bfloat16)

    def fetch(s, p):
        load_own(s, p).start()
        give(s, p).start()

    def arrive(s, p, first):
        load_own(s, p).wait()
        if held is not None:
            give(s, p).wait()
        else:
            give(s, p).wait_recv()
        if not first:
            ring(s - 1, p).wait_recv()

    def add(s, p, first=False):
        arrive(s, p, first)

        def body(h, row):
            k, d, _, _ = parts[p]
            w_out[k][tile(p, at.turn(d, s), at.c, h, row)] = total(s, p, h, row, first)

        by_rows(p, body)
        ring(s, p).start()
        if not first:
            ring(s - 1, p).wait_send()

    def load_state(p, w, m, v):
        k, d, _, _ = parts[p]
        return [
            pltpu.make_async_copy(w[k].at[layers(p), rows_of(p, at.z, at.c)], wb[k].at[d, :, within(p)], sems.state.at[0, p]),
            pltpu.make_async_copy(m[k].at[layers(p), within(p)], m_out[k].at[layers(p), within(p)], sems.state.at[1, p]),
            pltpu.make_async_copy(v[k].at[layers(p), within(p)], v_out[k].at[layers(p), within(p)], sems.state.at[2, p]),
        ]

    def update(p, w, m, v):
        arrive(at.last, p, False)
        for copy in load_state(p, w, m, v):
            copy.wait()

        def body(h, row):
            k, d, start, _ = parts[p]
            grad = total(at.last, p, h, row, False).astype(jnp.float32)
            here = pl.ds(pl.multiple_of(start + row, ROWS), ROWS)
            state = d * half[k] + h, here
            old = wb[k][d, h, here].astype(jnp.float32)
            new = adamw(old, m_out[k][state], v_out[k][state], grad)
            w_out[k][tile(p, at.z, at.c, h, row)], m_out[k][state], v_out[k][state] = new

        by_rows(p, body)

    def reduce_middle(first_step):
        @pl.loop(first_step, at.last - 1)
        def _(s):
            for p in e.parts:
                add(s, p)
                fetch(s + 2, p)

    def may_land(which, p):
        pl.semaphore_signal(sems.clear.at[which, p], inc=1, device_id=at.behind[parts[p][1]])

    def gather_after(which, t, p):
        pl.semaphore_wait(sems.clear.at[which, p], 1)
        gather(t, p).start()

    def may_side(p):
        pl.semaphore_signal(sems.free.at[p], inc=1, device_id=at.partner)

    def first_side(p):
        pl.semaphore_wait(sems.free.at[p], 1)
        side(0, p).start()

    def onward(t, p, which=None):
        gather(t - 1, p).wait_recv()
        if which is None:
            gather(t, p).start()
        else:
            gather_after(which, t, p)
        side(t, p).start()

    def end_gather():
        @pl.loop(0, at.last)
        def _(t):
            for p in e.parts:
                gather(t, p).wait_send()
                side(t, p).wait_send()
                side(t, p).wait_recv()

        for p in e.parts:
            side(at.last, p).wait_send()
            side(at.last, p).wait_recv()

    def end_give():
        @pl.loop(0, at.chips)
        def _(s):
            for p in e.parts:
                give(s, p).wait_send()

    for one in (
        fetch, add, load_state, update, reduce_middle, may_land, gather_after, may_side, first_side, onward, end_gather, end_give,
        ring, gather, side, slot, layers, within,
    ):
        setattr(e, one.__name__, one)
    return e


RING = ("own", "give_send", "give_recv", "ring_send", "ring_recv", "state")
GATHER = ("ag_send", "ag_recv", "side_send", "side_recv", "free", "clear")


def semaphores(chips, count, names):
    dma, plain = pltpu.SemaphoreType.DMA, pltpu.SemaphoreType.REGULAR
    full, less = (dma((chips, count)), dma((chips - 1, count)))
    shape = dict(
        own=dma((2, count)), give_send=full, give_recv=full, ring_send=less, ring_recv=less, state=dma((3, count)),
        ag_send=less, ag_recv=less, side_send=full, side_recv=full, free=plain((count,)), clear=plain((2, count)),
    )
    return [shape[name] for name in names]


def taker(refs):
    refs = list(refs)

    def take(number):
        head = refs[:number]
        del refs[:number]
        return head

    return take


def first_kernel(chips, early, parts, late_parts, *refs):
    take = taker(refs)
    late = LATE
    g, late_g, w, late_w = take(early), take(late), take(early), take(late)
    m, late_m, v, late_v = take(early), take(late), take(early), take(late)
    w_out, m_out, v_out = (take(early) for _ in range(3))
    held, new_w, new_m, new_v = (take(late) for _ in range(4))
    own, wb = take(early), take(early)
    late_own, late_wb, work, work_m, work_v = (take(late) for _ in range(5))
    sems = types.SimpleNamespace(**dict(zip(RING + GATHER, take(len(RING + GATHER)))))
    late_sems = types.SimpleNamespace(**dict(zip(RING, take(len(RING)))))
    hold_send, hold_recv, store = take(3)
    at = place(chips)
    last = at.last
    a = engine(at, parts, g, w_out, m_out, v_out, own, wb, sems)
    b = engine(at, late_parts, late_g, work, work_m, work_v, late_own, late_wb, late_sems, held)

    def hold(s, k, d):
        half, rows = held[k].shape[2:4]
        where = pl.ds(pl.multiple_of((at.turn(d, s) * CORES + at.other) * rows, rows), rows)
        return pltpu.make_async_remote_copy(
            late_g[k].at[0, pl.ds(d * half, half), where],
            held[k].at[s, d],
            hold_send.at[s, k, d],
            hold_recv.at[s, k, d],
            device_id=at.partner,
        )

    pairs = [(k, d) for k in range(late) for d in range(WAYS)]

    def store_new(p):
        k, d, _, _ = late_parts[p]
        rows = b.within(p)
        return [
            pltpu.make_async_copy(b.slot(p, at.z, at.c), new_w[k].at[d, :, rows], store.at[0, p]),
            pltpu.make_async_copy(work_m[k].at[b.layers(p), rows], new_m[k].at[b.layers(p), rows], store.at[1, p]),
            pltpu.make_async_copy(work_v[k].at[b.layers(p), rows], new_v[k].at[b.layers(p), rows], store.at[2, p]),
        ]

    barrier = pltpu.get_barrier_semaphore()
    for device in (*at.ahead, at.partner):
        pl.semaphore_signal(barrier, inc=1, device_id=device)
    pl.semaphore_wait(barrier, 3)
    for s in range(2):
        for p in a.parts:
            a.fetch(s, p)
    for p in a.parts:
        a.add(0, p, True)
        a.fetch(2, p)
    for p in a.parts:
        for copy in a.load_state(p, w, m, v):
            copy.start()
    a.reduce_middle(1)
    for p in a.parts:
        a.add(last - 1, p)
        a.may_land(0, p)
    for p in a.parts:
        a.update(p, w, m, v)
        a.gather_after(0, 0, p)
        a.may_side(p)
        if p:
            a.first_side(p - 1)
    a.first_side(len(parts) - 1)
    for p in a.parts:
        a.ring(last - 1, p).wait_send()
        a.may_land(1, p)

    @pl.loop(1, last - 1)
    def _(t):
        for p in a.parts:
            a.onward(t, p)
        for k, d in pairs:
            hold(t - 1, k, d).start()

    for s in range(last - 2, chips):
        for k, d in pairs:
            hold(s, k, d).start()
    for p in a.parts:
        a.onward(last - 1, p, 1)

    @pl.when(at.c == 1)
    def _():
        for s in range(2):
            for k, d in pairs:
                hold(s, k, d).wait_recv()
            for p in b.parts:
                b.fetch(s, p)
        for p in b.parts:
            b.add(0, p, True)
        for k, d in pairs:
            hold(2, k, d).wait_recv()
        for p in b.parts:
            b.fetch(2, p)

    for p in a.parts:
        a.gather(last - 1, p).wait_recv()
        a.side(last, p).start()

    @pl.loop(3, chips)
    def _(s):
        for k, d in pairs:
            hold(s, k, d).wait_recv()

    @pl.when(at.c == 1)
    def _():
        for p in b.parts:
            for copy in b.load_state(p, late_w, late_m, late_v):
                copy.start()
        b.reduce_middle(1)
        for p in b.parts:
            b.add(last - 1, p)
        for p in b.parts:
            b.update(p, late_w, late_m, late_v)
            for copy in store_new(p):
                copy.start()
        for p in b.parts:
            b.ring(last - 1, p).wait_send()
            for copy in store_new(p):
                copy.wait()

    @pl.when(at.c == 0)
    def _():
        for s in range(3):
            for k, d in pairs:
                hold(s, k, d).wait_recv()

    a.end_give()
    a.end_gather()

    @pl.loop(0, chips)
    def _(s):
        for k, d in pairs:
            hold(s, k, d).wait_send()


def second_kernel(chips, parts, *refs):
    take = taker(refs)
    count = LATE
    g, w, m, v, held, new_w, new_m, new_v = (take(count) for _ in range(8))
    take(1)
    w_out, m_out, v_out = (take(count) for _ in range(3))
    own, wb = take(count), take(count)
    sems = types.SimpleNamespace(**dict(zip(RING + GATHER, take(len(RING + GATHER)))))
    at = place(chips)
    last = at.last
    a = engine(at, parts, g, w_out, m_out, v_out, own, wb, sems, held)

    def bring(p):
        k, d, _, _ = parts[p]
        rows = a.within(p)
        return [
            pltpu.make_async_copy(new_w[k].at[d, :, rows], a.slot(p, at.z, at.c), sems.state.at[0, p]),
            pltpu.make_async_copy(new_m[k].at[a.layers(p), rows], m_out[k].at[a.layers(p), rows], sems.state.at[1, p]),
            pltpu.make_async_copy(new_v[k].at[a.layers(p), rows], v_out[k].at[a.layers(p), rows], sems.state.at[2, p]),
        ]

    barrier = pltpu.get_barrier_semaphore()
    for device in at.ahead:
        pl.semaphore_signal(barrier, inc=1, device_id=device)

    @pl.when(at.c == 0)
    def _():
        for s in range(2):
            for p in a.parts:
                a.fetch(s, p)
        pl.semaphore_wait(barrier, 2)
        pl.semaphore_signal(barrier, inc=1, device_id=at.partner)
        for p in a.parts:
            a.add(0, p, True)
            a.fetch(2, p)
        for p in a.parts:
            for copy in a.load_state(p, w, m, v):
                copy.start()
        a.reduce_middle(1)
        for p in a.parts:
            a.add(last - 1, p)
            a.may_land(0, p)
        for p in a.parts:
            a.update(p, w, m, v)
            a.gather_after(0, 0, p)
        for p in a.parts:
            a.ring(last - 1, p).wait_send()
            a.may_land(1, p)
        pl.semaphore_wait(barrier, 1)

    @pl.when(at.c == 1)
    def _():
        for p in a.parts:
            for copy in bring(p):
                copy.start()
        pl.semaphore_wait(barrier, 3)
        pl.semaphore_signal(barrier, inc=1, device_id=at.partner)
        for p in a.parts:
            for which in range(2):
                a.may_land(which, p)
        for p in a.parts:
            for copy in bring(p):
                copy.wait()
            a.gather_after(0, 0, p)

    for p in a.parts:
        a.may_side(p)
    for p in a.parts:
        a.first_side(p)

    @pl.loop(1, last - 1)
    def _(t):
        for p in a.parts:
            a.onward(t, p)

    for p in a.parts:
        a.onward(last - 1, p, 1)
    for p in a.parts:
        a.gather(last - 1, p).wait_recv()
        a.side(last, p).start()
    a.end_gather()


def settle(count, *refs):
    sources, targets, sem = refs[:count], refs[count : 2 * count], refs[-1]
    copies = [
        pltpu.make_async_copy(source.at[layer], target.at[layer], sem.at[i, layer])
        for i, (source, target) in enumerate(zip(sources, targets))
        for layer in range(source.shape[0])
    ]
    for copy in copies:
        copy.start()
    refs[2 * count][...] = jnp.zeros_like(refs[2 * count])
    for copy in copies:
        copy.wait()


def solution(mesh):
    chips = mesh.shape["dp"] // CORES
    any_of, vmem = (pl.BlockSpec(memory_space=space) for space in (pl.ANY, pltpu.VMEM))
    dma = pltpu.SemaphoreType.DMA
    mib = 1024 * 1024

    def in_hbm(arrays):
        return [pltpu.with_memory_space_constraint(one, pltpu.HBM) for one in arrays]

    def out(arrays):
        layers = max(one.shape[0] for one in arrays)
        shapes = [jax.ShapeDtypeStruct(one.shape, one.dtype) for one in arrays]
        *whole, token = pl.pallas_call(
            functools.partial(settle, len(arrays)),
            out_shape=[*shapes, jax.ShapeDtypeStruct((8, 128), jnp.float32)],
            in_specs=[vmem] * len(arrays),
            out_specs=[any_of] * len(arrays) + [vmem],
            scratch_shapes=[dma((len(arrays), layers))],
            compiler_params=pltpu.CompilerParams(vmem_limit_bytes=2 * mib),
        )(*(pltpu.with_memory_space_constraint(one, pltpu.VMEM) for one in arrays))
        return whole, token

    def step(*arrays):
        terms, weights, m, v = (arrays[i : i + 3] for i in (0, 3, 6, 9))
        early = len(weights) - LATE
        shapes = [(one.shape[0] // WAYS, *one.shape[1:]) for one in m]
        parts, late_parts = parts_of(m[:early], 1), parts_of(m[early:], PIECES)

        def slots(some, number, dtype=jnp.bfloat16):
            return [pltpu.VMEM((*number, *one), dtype) for one in some]

        late_shapes = shapes[early:]
        results = pl.pallas_call(
            functools.partial(first_kernel, chips, early, parts, late_parts),
            out_shape=[
                *(pltpu.VMEM(one.shape, one.dtype) for one in (*weights[:early], *m[:early], *v[:early])),
                *(pltpu.HBM((chips, WAYS, *one), jnp.bfloat16) for one in late_shapes),
                *(pltpu.HBM((WAYS, *one), jnp.bfloat16) for one in late_shapes),
                *(pltpu.HBM(one.shape, one.dtype) for one in (*m[early:], *v[early:])),
            ],
            in_specs=[any_of] * len(arrays),
            out_specs=[vmem] * (3 * early) + [any_of] * (4 * LATE),
            scratch_shapes=[
                *slots(shapes[:early], (2, WAYS)),
                *slots(shapes[:early], (WAYS,)),
                *slots(late_shapes, (2, WAYS)),
                *slots(late_shapes, (WAYS,)),
                *(pltpu.VMEM(one.shape, one.dtype) for one in (*weights[early:], *m[early:], *v[early:])),
                *semaphores(chips, len(parts), RING + GATHER),
                *semaphores(chips, len(late_parts), RING),
                dma((chips, LATE, WAYS)),
                dma((chips, LATE, WAYS)),
                dma((3, len(late_parts))),
            ],
            compiler_params=pltpu.CompilerParams(collective_id=0, has_side_effects=True, vmem_limit_bytes=24 * mib),
        )(*in_hbm(arrays))
        (w1, m1, v1), rest = (results[i : i + early] for i in (0, early, 2 * early)), results[3 * early :]
        done, token = out([*w1, *m1, *v1])
        late = [one for kind in (terms, weights, m, v) for one in kind[early:]]
        results = pl.pallas_call(
            functools.partial(second_kernel, chips, late_parts),
            out_shape=[pltpu.VMEM(one.shape, one.dtype) for one in (*weights[early:], *m[early:], *v[early:])],
            in_specs=[any_of] * (len(late) + len(rest) + 1),
            out_specs=[vmem] * (3 * LATE),
            scratch_shapes=[
                *slots(late_shapes, (2, WAYS)),
                *slots(late_shapes, (WAYS,)),
                *semaphores(chips, len(late_parts), RING + GATHER),
            ],
            compiler_params=pltpu.CompilerParams(collective_id=1, has_side_effects=True, vmem_limit_bytes=8 * mib),
        )(*in_hbm([*late, *rest, token]))
        then, _ = out(results)
        return tuple(
            one
            for i in range(3)
            for one in (*done[i * early : (i + 1) * early], *then[i * LATE : (i + 1) * LATE])
        )

    all_of, sharded = P(None, None, None), P(None, "dp", None)
    return jax.shard_map(
        step,
        mesh=mesh,
        in_specs=(P(("rep", "dp"), None, None, None),) * 3 + (all_of,) * 3 + (sharded,) * 6,
        out_specs=(P("rep", None, None),) * 3 + (P("rep", "dp", None),) * 6,
        check_vma=False,
    )
```

time: 475 us -> 349 us (0.73)
  waiting for transfers between devices: 425 us -> 0 us
  Pallas kernels: 0 us -> 348 us
  local copies, waits for them, and re-layouts: 24 us -> 0.59 us
  between operations: 14.2 us -> 0.68 us
  other arithmetic: 11.6 us -> 0 us
    pallas_call x0 -> x4, Pallas kernels: none -> 348 us  [the longest x1 267 us: step(): pl.pallas_call(functools.partial(first_kernel, chips, early, parts, late_...]
    reduce_scatter x3 -> x0, waiting for transfers between devices: 218 us -> none  [step(): lax.psum_scatter(t[0], 'dp', scatter_dimension=1, tiled=True)]
    all_gather x3 -> x0, waiting for transfers between devices: 204 us -> none  [step(): whole = [lax.all_gather(one[0], 'dp', axis=1, tiled=True) for one in new]]
    unnamed x19 -> x2, local copies, waits for them, and re-layouts: 24 us -> 0.59 us
    convert_element_type x3 -> x0, other arithmetic: 11.6 us -> none  [adamw(): return ((w - 0.02 * step).astype(jnp.bfloat16), m, v)]
  transfers between devices with their start and end apart: 6 -> 0, of which waited for: 6 -> 0; matrix products, arithmetic and copies ran while one was open for 2% -> 0% of each run, Pallas kernels for 0% -> 0%
where the time goes in v3:
time: 349 us
  Pallas kernels  348 us (100%)
    pallas_call x1, Pallas kernels, step(): pl.pallas_call(functools.partial(first_kernel, chips, early, parts, late_...  267 us
    pallas_call x1, Pallas kernels, step(): pl.pallas_call(functools.partial(second_kernel, chips, late_parts), out_s...  65.7 us
    pallas_call x2, Pallas kernels, out(): pl.pallas_call(functools.partial(settle, len(arrays)), out_shape=[*shapes...  15.4 us

profile of v3, /device:TPU:21, one launch (start us, length us, event | category | flops | bytes accessed | tf_op | source)
XLA Modules:
  0.0 349.1 jit_solution(2830276595146540881)
XLA Ops:
  0.6 266.7 %shard_map.187 = (bf16[2,1024,2816]{2,1,0:T(8,128)(2,1)S(1)}, bf16[2,1024,2816]{2,1,0:T(8,128)(2,1)S(1)}, f32[2,64,2816]{2,1,0:T(8,128)S(1)}, f32[2,64,2816]{2,1...) custom-call(bf16[1,2,1024,2816]{3,2,1,0:T(8,128)(2,1)} %refs_0_.2, ...), custom_call_target="tpu_custom_call" | custom-call | tf_op jit(solution)/shard_map/pallas_call | solution.py:531
  267.4 9.6 %shard_map.188 = (bf16[2,1024,2816]{2,1,0:T(8,128)(2,1)}, bf16[2,1024,2816]{2,1,0:T(8,128)(2,1)}, f32[2,64,2816]{2,1,0:T(8,128)}, f32[2,64,2816]{2,1,0:T(8,128)}...) custom-call(bf16[2,1024,2816]{2,1,0:T(8,128)(2,1)S(1)} %get-tuple-element.32.refs_0_, ...), custom_call_target="tpu_custom_call" | custom-call | tf_op jit(solution)/shard_map/pallas_call | solution.py:511
  277.0 0.0 copy-start
  277.0 0.6 copy-done
  277.6 65.7 %shard_map.189 = (bf16[2,2816,1024]{2,1,0:T(8,128)(2,1)S(1)}, f32[2,176,1024]{2,1,0:T(8,128)S(1)}, f32[2,176,1024]{2,1,0:T(8,128)S(1)}) custom-call(bf16[1,2,2816,1024]{3,2,1,0:T(8,128)(2,1)} %refs_0_.3, bf16[2,2816,1024]{2,1,0:T(8,128)(2,1)} %refs_1_.3, f32[2,176,1024]{2,1,0:T(8,128)} %refs_2_.3, f32[2,176,1024]{2,1,0:T(8,128)} %refs_3_.3, ...), custom_call_target="tpu_custom_call" | custom-call | tf_op jit(solution)/shard_map/pallas_call | solution.py:558
  343.3 5.8 %shard_map.190 = (bf16[2,2816,1024]{2,1,0:T(8,128)(2,1)}, f32[2,176,1024]{2,1,0:T(8,128)}, f32[2,176,1024]{2,1,0:T(8,128)}, f32[8,128]{1,0:T(8,128)}) custom-call(bf16[2,2816,1024]{2,1,0:T(8,128)(2,1)S(1)} %get-tuple-element.45.refs_0_, f32[2,176,1024]{2,1,0:T(8,128)S(1)} %get-tuple-element.46.refs_1_, f32[2,176,1024]{2,1,0:T(8,128)S(1)} %get-tuple-element.47.refs_2_), custom_call_target="tpu_custom_call" | custom-call | tf_op jit(solution)/shard_map/pallas_call | solution.py:511
Async XLA Ops:
  277.0 0.6 copy-start

commit v4 on v3

--- a/solution.py
+++ b/solution.py
@@ -73,31 +73,57 @@
     def slot(p, chip_of, core):
         return w_out[parts[p][0]].at[layers(p), rows_of(p, chip_of, core)]
 
-    def load_own(s, p):
-        k, d, _, _ = parts[p]
-        here = g[k].at[0, layers(p), rows_of(p, at.turn(d, s), at.c)]
-        return pltpu.make_async_copy(here, own[k].at[s % 2, d, :, within(p)], sems.own.at[s % 2, p])
+    ways = range(WAYS)
+    opens = [all(parts[q][0] != part[0] for q in range(p)) for p, part in enumerate(parts)]
+    closes = [all(parts[q][0] != part[0] for q in range(p + 1, len(parts))) for p, part in enumerate(parts)]
+
+    def all_of(k, d, chip_of, core):
+        start = pl.multiple_of((chip_of * CORES + core) * block_rows[k], block_rows[k])
+        return pl.ds(d * half[k], half[k]), pl.ds(start, block_rows[k])
+
+    def blocks(k, number):
+        return w_out[k].at[:, pl.ds(0, number * block_rows[k])]
+
+    def wait_all(ref, sem):
+        pltpu.make_async_copy(ref, ref, sem).wait()
+
+    def load_own(s, k):
+        for d in ways:
+            here = (0, *all_of(k, d, at.turn(d, s), at.c))
+            pltpu.make_async_copy(g[k].at[here], own[k].at[s % 2, d], sems.own.at[s % 2, k]).start()
 
     def give(s, p):
         k, d, _, _ = parts[p]
-        if held is not None:
-            kept = held[k].at[s, d, :, within(p)]
-            return pltpu.make_async_copy(kept, slot(p, at.turn(d, s), at.c), sems.give_recv.at[s, p])
         where = rows_of(p, at.turn(d, s), at.other)
         return pltpu.make_async_remote_copy(
             g[k].at[0, layers(p), where],
             w_out[k].at[layers(p), where],
-            sems.give_send.at[s, p],
-            sems.give_recv.at[s, p],
+            sems.first_send.at[p],
+            sems.first_recv.at[p],
             device_id=at.partner,
         )
+
+    def give_all(s, k):
+        for d in ways:
+            if held is not None:
+                slot_of = w_out[k].at[all_of(k, d, at.turn(d, s), at.c)]
+                pltpu.make_async_copy(held[k].at[s, d], slot_of, sems.kept.at[s % 2, k]).start()
+            else:
+                where = all_of(k, d, at.turn(d, s), at.other)
+                pltpu.make_async_remote_copy(
+                    g[k].at[(0, *where)],
+                    w_out[k].at[where],
+                    sems.give_send.at[k],
+                    sems.give_recv.at[s, k],
+                    device_id=at.partner,
+                ).start()
 
     def ring(s, p):
         d = parts[p][1]
         return pltpu.make_async_remote_copy(
             slot(p, at.turn(d, s), at.c),
             slot(p, at.turn(d, s), at.other),
-            sems.ring_send.at[s, p],
+            sems.ring_send.at[s % 2, p],
             sems.ring_recv.at[s, p],
             device_id=at.ahead[d],
         )
@@ -108,12 +134,13 @@
     def gather(t, p):
         here = travelling(t, p)
         return pltpu.make_async_remote_copy(
-            here, here, sems.ag_send.at[t, p], sems.ag_recv.at[t, p], device_id=at.ahead[parts[p][1]]
+            here, here, sems.ag_send.at[parts[p][0]], sems.ag_recv.at[t, p], device_id=at.ahead[parts[p][1]]
         )
 
     def side(t, p):
         here = travelling(t, p)
-        return pltpu.make_async_remote_copy(here, here, sems.side_send.at[t, p], sems.side_recv.at[t, p], device_id=at.partner)
+        k = parts[p][0]
+        return pltpu.make_async_remote_copy(here, here, sems.side_send.at[k], sems.side_recv.at[k], device_id=at.partner)
 
     def by_rows(p, body):
         for h in range(half[parts[p][0]]):
@@ -135,21 +162,27 @@
             so_far = so_far + w_out[k][tile(p, at.turn(d, s), at.other, h, row)].astype(jnp.float32)
         return so_far.astype(jnp.bfloat16)
 
-    def fetch(s, p):
-        load_own(s, p).start()
-        give(s, p).start()
+    def fetch(s, k):
+        load_own(s, k)
+        give_all(s, k)
 
     def arrive(s, p, first):
-        load_own(s, p).wait()
-        if held is not None:
-            give(s, p).wait()
-        else:
+        k = parts[p][0]
+        if opens[p]:
+            wait_all(own[k].at[s % 2], sems.own.at[s % 2, k])
+            if held is not None:
+                wait_all(blocks(k, 1), sems.kept.at[s % 2, k])
+            elif not first:
+                wait_all(blocks(k, 1), sems.give_recv.at[s, k])
+        if first and held is None:
             give(s, p).wait_recv()
         if not first:
             ring(s - 1, p).wait_recv()
 
-    def add(s, p, first=False):
+    def add(s, p, first=False, then=None):
         arrive(s, p, first)
+        if then is not None:
+            then()
 
         def body(h, row):
             k, d, _, _ = parts[p]
@@ -160,18 +193,18 @@
         if not first:
             ring(s - 1, p).wait_send()
 
-    def load_state(p, w, m, v):
-        k, d, _, _ = parts[p]
-        return [
-            pltpu.make_async_copy(w[k].at[layers(p), rows_of(p, at.z, at.c)], wb[k].at[d, :, within(p)], sems.state.at[0, p]),
-            pltpu.make_async_copy(m[k].at[layers(p), within(p)], m_out[k].at[layers(p), within(p)], sems.state.at[1, p]),
-            pltpu.make_async_copy(v[k].at[layers(p), within(p)], v_out[k].at[layers(p), within(p)], sems.state.at[2, p]),
-        ]
-
-    def update(p, w, m, v):
+    def load_state(k, w, m, v):
+        for d in ways:
+            here = all_of(k, d, at.z, at.c)
+            pltpu.make_async_copy(w[k].at[here], wb[k].at[d], sems.state.at[0, k]).start()
+        pltpu.make_async_copy(m[k], m_out[k], sems.state.at[1, k]).start()
+        pltpu.make_async_copy(v[k], v_out[k], sems.state.at[2, k]).start()
+
+    def update(p):
         arrive(at.last, p, False)
-        for copy in load_state(p, w, m, v):
-            copy.wait()
+        if opens[p]:
+            for i, ref in enumerate((wb, m_out, v_out)):
+                wait_all(ref[parts[p][0]], sems.state.at[i, parts[p][0]])
 
         def body(h, row):
             k, d, start, _ = parts[p]
@@ -189,7 +222,8 @@
         def _(s):
             for p in e.parts:
                 add(s, p)
-                fetch(s + 2, p)
+                if closes[p]:
+                    fetch(s + 2, parts[p][0])
 
     def may_land(which, p):
         pl.semaphore_signal(sems.clear.at[which, p], inc=1, device_id=at.behind[parts[p][1]])
@@ -214,43 +248,44 @@
         side(t, p).start()
 
     def end_gather():
-        @pl.loop(0, at.last)
-        def _(t):
-            for p in e.parts:
-                gather(t, p).wait_send()
-                side(t, p).wait_send()
-                side(t, p).wait_recv()
-
+        for k in range(len(w_out)):
+            wait_all(blocks(k, at.last), sems.ag_send.at[k])
+            wait_all(blocks(k, at.chips), sems.side_send.at[k])
+            wait_all(blocks(k, at.chips), sems.side_recv.at[k])
+
+    def end_give():
+        for k in range(len(w_out)):
+            wait_all(blocks(k, at.last), sems.give_send.at[k])
         for p in e.parts:
-            side(at.last, p).wait_send()
-            side(at.last, p).wait_recv()
-
-    def end_give():
-        @pl.loop(0, at.chips)
-        def _(s):
-            for p in e.parts:
-                give(s, p).wait_send()
+            give(0, p).wait_send()
 
     for one in (
-        fetch, add, load_state, update, reduce_middle, may_land, gather_after, may_side, first_side, onward, end_gather, end_give,
+        fetch, load_own, give, give_all, add, load_state, wait_all, all_of, update, reduce_middle, may_land, gather_after, may_side, first_side, onward, end_gather, end_give,
         ring, gather, side, slot, layers, within,
     ):
         setattr(e, one.__name__, one)
     return e
 
 
-RING = ("own", "give_send", "give_recv", "ring_send", "ring_recv", "state")
+GIVE = ("first_send", "first_recv", "give_send", "give_recv")
+KEPT = ("kept",)
+RING = ("own", "ring_send", "ring_recv", "state")
 GATHER = ("ag_send", "ag_recv", "side_send", "side_recv", "free", "clear")
 
 
-def semaphores(chips, count, names):
+def semaphores(chips, count, weights, names):
     dma, plain = pltpu.SemaphoreType.DMA, pltpu.SemaphoreType.REGULAR
-    full, less = (dma((chips, count)), dma((chips - 1, count)))
     shape = dict(
-        own=dma((2, count)), give_send=full, give_recv=full, ring_send=less, ring_recv=less, state=dma((3, count)),
-        ag_send=less, ag_recv=less, side_send=full, side_recv=full, free=plain((count,)), clear=plain((2, count)),
+        first_send=dma((count,)), first_recv=dma((count,)), give_send=dma((weights,)), give_recv=dma((chips, weights)),
+        kept=dma((2, weights)), own=dma((2, weights)), ring_send=dma((2, count)), ring_recv=dma((chips - 1, count)),
+        state=dma((3, weights)), ag_send=dma((weights,)), ag_recv=dma((chips - 1, count)), side_send=dma((weights,)),
+        side_recv=dma((weights,)), free=plain((count,)), clear=plain((2, count)),
     )
     return [shape[name] for name in names]
+
+
+def named(names, refs):
+    return types.SimpleNamespace(**dict(zip(names, refs)))
 
 
 def taker(refs):
@@ -273,8 +308,7 @@
     held, new_w, new_m, new_v = (take(late) for _ in range(4))
     own, wb = take(early), take(early)
     late_own, late_wb, work, work_m, work_v = (take(late) for _ in range(5))
-    sems = types.SimpleNamespace(**dict(zip(RING + GATHER, take(len(RING + GATHER)))))
-    late_sems = types.SimpleNamespace(**dict(zip(RING, take(len(RING)))))
+    sems, late_sems = (named(names, take(len(names))) for names in (GIVE + RING + GATHER, KEPT + RING))
     hold_send, hold_recv, store = take(3)
     at = place(chips)
     last = at.last
@@ -287,41 +321,48 @@
         return pltpu.make_async_remote_copy(
             late_g[k].at[0, pl.ds(d * half, half), where],
             held[k].at[s, d],
-            hold_send.at[s, k, d],
-            hold_recv.at[s, k, d],
+            hold_send.at[k],
+            hold_recv.at[s, k],
             device_id=at.partner,
         )
 
     pairs = [(k, d) for k in range(late) for d in range(WAYS)]
+
+    def kept(s):
+        for k in range(late):
+            b.wait_all(held[k].at[s], hold_recv.at[s, k])
 
     def store_new(p):
         k, d, _, _ = late_parts[p]
         rows = b.within(p)
         return [
-            pltpu.make_async_copy(b.slot(p, at.z, at.c), new_w[k].at[d, :, rows], store.at[0, p]),
-            pltpu.make_async_copy(work_m[k].at[b.layers(p), rows], new_m[k].at[b.layers(p), rows], store.at[1, p]),
-            pltpu.make_async_copy(work_v[k].at[b.layers(p), rows], new_v[k].at[b.layers(p), rows], store.at[2, p]),
+            pltpu.make_async_copy(b.slot(p, at.z, at.c), new_w[k].at[d, :, rows], store.at[0, k]),
+            pltpu.make_async_copy(work_m[k].at[b.layers(p), rows], new_m[k].at[b.layers(p), rows], store.at[1, k]),
+            pltpu.make_async_copy(work_v[k].at[b.layers(p), rows], new_v[k].at[b.layers(p), rows], store.at[2, k]),
         ]
 
     barrier = pltpu.get_barrier_semaphore()
     for device in (*at.ahead, at.partner):
         pl.semaphore_signal(barrier, inc=1, device_id=device)
+    for s in range(2):
+        for k in range(early):
+            a.load_own(s, k)
     pl.semaphore_wait(barrier, 3)
-    for s in range(2):
-        for p in a.parts:
-            a.fetch(s, p)
+    for p in a.parts:
+        a.give(0, p).start()
+    for k in range(early):
+        a.give_all(1, k)
     for p in a.parts:
         a.add(0, p, True)
-        a.fetch(2, p)
-    for p in a.parts:
-        for copy in a.load_state(p, w, m, v):
-            copy.start()
+    for k in range(early):
+        a.fetch(2, k)
+        a.load_state(k, w, m, v)
     a.reduce_middle(1)
     for p in a.parts:
         a.add(last - 1, p)
         a.may_land(0, p)
     for p in a.parts:
-        a.update(p, w, m, v)
+        a.update(p)
         a.gather_after(0, 0, p)
         a.may_side(p)
         if p:
@@ -347,16 +388,14 @@
     @pl.when(at.c == 1)
     def _():
         for s in range(2):
-            for k, d in pairs:
-                hold(s, k, d).wait_recv()
-            for p in b.parts:
-                b.fetch(s, p)
+            kept(s)
+            for k in range(late):
+                b.fetch(s, k)
         for p in b.parts:
             b.add(0, p, True)
-        for k, d in pairs:
-            hold(2, k, d).wait_recv()
-        for p in b.parts:
-            b.fetch(2, p)
+        kept(2)
+        for k in range(late):
+            b.fetch(2, k)
 
     for p in a.parts:
         a.gather(last - 1, p).wait_recv()
@@ -364,39 +403,34 @@
 
     @pl.loop(3, chips)
     def _(s):
-        for k, d in pairs:
-            hold(s, k, d).wait_recv()
+        kept(s)
 
     @pl.when(at.c == 1)
     def _():
-        for p in b.parts:
-            for copy in b.load_state(p, late_w, late_m, late_v):
-                copy.start()
+        for k in range(late):
+            b.load_state(k, late_w, late_m, late_v)
         b.reduce_middle(1)
         for p in b.parts:
             b.add(last - 1, p)
         for p in b.parts:
-            b.update(p, late_w, late_m, late_v)
+            b.update(p)
             for copy in store_new(p):
                 copy.start()
         for p in b.parts:
             b.ring(last - 1, p).wait_send()
-            for copy in store_new(p):
-                copy.wait()
+        for k in range(late):
+            for i, ref in enumerate((new_w, new_m, new_v)):
+                b.wait_all(ref[k], store.at[i, k])
 
     @pl.when(at.c == 0)
     def _():
         for s in range(3):
-            for k, d in pairs:
-                hold(s, k, d).wait_recv()
+            kept(s)
 
     a.end_give()
     a.end_gather()
-
-    @pl.loop(0, chips)
-    def _(s):
-        for k, d in pairs:
-            hold(s, k, d).wait_send()
+    for k in range(late):
+        b.wait_all(held[k], hold_send.at[k])
 
 
 def second_kernel(chips, parts, *refs):
@@ -406,19 +440,17 @@
     take(1)
     w_out, m_out, v_out = (take(count) for _ in range(3))
     own, wb = take(count), take(count)
-    sems = types.SimpleNamespace(**dict(zip(RING + GATHER, take(len(RING + GATHER)))))
+    sems = named(KEPT + RING + GATHER, take(len(KEPT + RING + GATHER)))
     at = place(chips)
     last = at.last
     a = engine(at, parts, g, w_out, m_out, v_out, own, wb, sems, held)
 
-    def bring(p):
-        k, d, _, _ = parts[p]
-        rows = a.within(p)
-        return [
-            pltpu.make_async_copy(new_w[k].at[d, :, rows], a.slot(p, at.z, at.c), sems.state.at[0, p]),
-            pltpu.make_async_copy(new_m[k].at[a.layers(p), rows], m_out[k].at[a.layers(p), rows], sems.state.at[1, p]),
-            pltpu.make_async_copy(new_v[k].at[a.layers(p), rows], v_out[k].at[a.layers(p), rows], sems.state.at[2, p]),
-        ]
+    def bring(k):
+        for d in range(WAYS):
+            here = w_out[k].at[a.all_of(k, d, at.z, at.c)]
+            pltpu.make_async_copy(new_w[k].at[d], here, sems.state.at[0, k]).start()
+        pltpu.make_async_copy(new_m[k], m_out[k], sems.state.at[1, k]).start()
+        pltpu.make_async_copy(new_v[k], v_out[k], sems.state.at[2, k]).start()
 
     barrier = pltpu.get_barrier_semaphore()
     for device in at.ahead:
@@ -427,22 +459,21 @@
     @pl.when(at.c == 0)
     def _():
         for s in range(2):
-            for p in a.parts:
-                a.fetch(s, p)
+            for k in range(count):
+                a.fetch(s, k)
         pl.semaphore_wait(barrier, 2)
         pl.semaphore_signal(barrier, inc=1, device_id=at.partner)
         for p in a.parts:
             a.add(0, p, True)
-            a.fetch(2, p)
-        for p in a.parts:
-            for copy in a.load_state(p, w, m, v):
-                copy.start()
+        for k in range(count):
+            a.fetch(2, k)
+            a.load_state(k, w, m, v)
         a.reduce_middle(1)
         for p in a.parts:
             a.add(last - 1, p)
             a.may_land(0, p)
         for p in a.parts:
-            a.update(p, w, m, v)
+            a.update(p)
             a.gather_after(0, 0, p)
         for p in a.parts:
             a.ring(last - 1, p).wait_send()
@@ -451,17 +482,17 @@
 
     @pl.when(at.c == 1)
     def _():
-        for p in a.parts:
-            for copy in bring(p):
-                copy.start()
+        for k in range(count):
+            bring(k)
         pl.semaphore_wait(barrier, 3)
         pl.semaphore_signal(barrier, inc=1, device_id=at.partner)
         for p in a.parts:
             for which in range(2):
                 a.may_land(which, p)
-        for p in a.parts:
-            for copy in bring(p):
-                copy.wait()
+        for k in range(count):
+            for i, ref in enumerate((new_w, m_out, v_out)):
+                a.wait_all(ref[k], sems.state.at[i, k])
+        for p in a.parts:
             a.gather_after(0, 0, p)
 
     for p in a.parts:
@@ -544,11 +575,11 @@
                 *slots(late_shapes, (2, WAYS)),
                 *slots(late_shapes, (WAYS,)),
                 *(pltpu.VMEM(one.shape, one.dtype) for one in (*weights[early:], *m[early:], *v[early:])),
-                *semaphores(chips, len(parts), RING + GATHER),
-                *semaphores(chips, len(late_parts), RING),
-                dma((chips, LATE, WAYS)),
-                dma((chips, LATE, WAYS)),
-                dma((3, len(late_parts))),
+                *semaphores(chips, len(parts), early, GIVE + RING + GATHER),
+                *semaphores(chips, len(late_parts), LATE, KEPT + RING),
+                dma((LATE,)),
+                dma((chips, LATE)),
+                dma((3, LATE)),
             ],
             compiler_params=pltpu.CompilerParams(collective_id=0, has_side_effects=True, vmem_limit_bytes=24 * mib),
         )(*in_hbm(arrays))
@@ -563,10 +594,10 @@
             scratch_shapes=[
                 *slots(late_shapes, (2, WAYS)),
                 *slots(late_shapes, (WAYS,)),
-                *semaphores(chips, len(late_parts), RING + GATHER),
+                *semaphores(chips, len(late_parts), LATE, KEPT + RING + GATHER),
             ],
             compiler_params=pltpu.CompilerParams(collective_id=1, has_side_effects=True, vmem_limit_bytes=8 * mib),
-        )(*in_hbm([*late, *rest, token]))
+        )(*in_hbm([*late, *rest]), token)
         then, _ = out(results)
         return tuple(
             one

time: 349 us -> 346 us (level)
  no operation moved by 1% of the time
where the time goes in v4:
time: 346 us
  Pallas kernels  345 us (100%)
    pallas_call x1, Pallas kernels, step(): pl.pallas_call(functools.partial(first_kernel, chips, early, parts, late_...  267 us
    pallas_call x1, Pallas kernels, step(): pl.pallas_call(functools.partial(second_kernel, chips, late_parts), out_s...  62.9 us
    pallas_call x2, Pallas kernels, out(): pl.pallas_call(functools.partial(settle, len(arrays)), out_shape=[*shapes...  15.4 us

profile of v4, /device:TPU:21, one launch (start us, length us, event | category | flops | bytes accessed | tf_op | source)
XLA Modules:
  0.0 345.6 jit_solution(10660195579842685771)
XLA Ops:
  0.6 266.7 %shard_map.187 = (bf16[2,1024,2816]{2,1,0:T(8,128)(2,1)S(1)}, bf16[2,1024,2816]{2,1,0:T(8,128)(2,1)S(1)}, f32[2,64,2816]{2,1,0:T(8,128)S(1)}, f32[2,64,2816]{2,1...) custom-call(bf16[1,2,1024,2816]{3,2,1,0:T(8,128)(2,1)} %refs_0_.2, ...), custom_call_target="tpu_custom_call" | custom-call | tf_op jit(solution)/shard_map/pallas_call | solution.py:562
  267.4 9.6 %shard_map.188 = (bf16[2,1024,2816]{2,1,0:T(8,128)(2,1)}, bf16[2,1024,2816]{2,1,0:T(8,128)(2,1)}, f32[2,64,2816]{2,1,0:T(8,128)}, f32[2,64,2816]{2,1,0:T(8,128)}...) custom-call(bf16[2,1024,2816]{2,1,0:T(8,128)(2,1)S(1)} %get-tuple-element.32.refs_0_, ...), custom_call_target="tpu_custom_call" | custom-call | tf_op jit(solution)/shard_map/pallas_call | solution.py:542
  277.0 62.9 %shard_map.189 = (bf16[2,2816,1024]{2,1,0:T(8,128)(2,1)S(1)}, f32[2,176,1024]{2,1,0:T(8,128)S(1)}, f32[2,176,1024]{2,1,0:T(8,128)S(1)}) custom-call(bf16[1,2,2816,1024]{3,2,1,0:T(8,128)(2,1)} %refs_0_.3, bf16[2,2816,1024]{2,1,0:T(8,128)(2,1)} %refs_1_.3, f32[2,176,1024]{2,1,0:T(8,128)} %refs_2_.3, f32[2,176,1024]{2,1,0:T(8,128)} %refs_3_.3, ...), custom_call_target="tpu_custom_call" | custom-call | tf_op jit(solution)/shard_map/pallas_call | solution.py:589
  339.8 5.8 %shard_map.190 = (bf16[2,2816,1024]{2,1,0:T(8,128)(2,1)}, f32[2,176,1024]{2,1,0:T(8,128)}, f32[2,176,1024]{2,1,0:T(8,128)}, f32[8,128]{1,0:T(8,128)}) custom-call(bf16[2,2816,1024]{2,1,0:T(8,128)(2,1)S(1)} %get-tuple-element.45.refs_0_, f32[2,176,1024]{2,1,0:T(8,128)S(1)} %get-tuple-element.46.refs_1_, f32[2,176,1024]{2,1,0:T(8,128)S(1)} %get-tuple-element.47.refs_2_), custom_call_target="tpu_custom_call" | custom-call | tf_op jit(solution)/shard_map/pallas_call | solution.py:542

commit v5 on v4

--- a/solution.py
+++ b/solution.py
@@ -12,7 +12,8 @@
 ROWS = 16
 WAYS = 2
 LATE = 1
-PIECES = 4
+FIRST = (1, 3)
+PIECES = (1, 1, 1, 1)
 
 
 def adamw(w, m, v, g):
@@ -22,14 +23,19 @@
     return (w - 0.02 * step).astype(jnp.bfloat16), m, v
 
 
-def cut(rows, pieces):
+def cut(rows, shares):
     tiles = rows // ROWS
-    ends = [tiles * i // pieces * ROWS for i in range(pieces + 1)]
+    ends = [tiles * sum(shares[:i]) // sum(shares) * ROWS for i in range(len(shares) + 1)]
     return [(a, b - a) for a, b in zip(ends, ends[1:]) if b > a]
 
 
-def parts_of(state, pieces):
-    return [(k, d, *piece) for k, one in enumerate(state) for piece in cut(one.shape[-2], pieces) for d in range(WAYS)]
+def parts_of(state, shares):
+    return [
+        (k, d, *piece)
+        for k, (one, some) in enumerate(zip(state, shares))
+        for piece in cut(one.shape[-2], some)
+        for d in range(WAYS)
+    ]
 
 
 def place(chips):
@@ -134,7 +140,7 @@
     def gather(t, p):
         here = travelling(t, p)
         return pltpu.make_async_remote_copy(
-            here, here, sems.ag_send.at[parts[p][0]], sems.ag_recv.at[t, p], device_id=at.ahead[parts[p][1]]
+            here, here, sems.ag_send.at[parts[p][0]], sems.ring_recv.at[t, p], device_id=at.ahead[parts[p][1]]
         )
 
     def side(t, p):
@@ -270,7 +276,7 @@
 GIVE = ("first_send", "first_recv", "give_send", "give_recv")
 KEPT = ("kept",)
 RING = ("own", "ring_send", "ring_recv", "state")
-GATHER = ("ag_send", "ag_recv", "side_send", "side_recv", "free", "clear")
+GATHER = ("ag_send", "side_send", "side_recv", "free", "clear")
 
 
 def semaphores(chips, count, weights, names):
@@ -278,7 +284,7 @@
     shape = dict(
         first_send=dma((count,)), first_recv=dma((count,)), give_send=dma((weights,)), give_recv=dma((chips, weights)),
         kept=dma((2, weights)), own=dma((2, weights)), ring_send=dma((2, count)), ring_recv=dma((chips - 1, count)),
-        state=dma((3, weights)), ag_send=dma((weights,)), ag_recv=dma((chips - 1, count)), side_send=dma((weights,)),
+        state=dma((3, weights)), ag_send=dma((weights,)), side_send=dma((weights,)),
         side_recv=dma((weights,)), free=plain((count,)), clear=plain((2, count)),
     )
     return [shape[name] for name in names]
@@ -553,7 +559,7 @@
         terms, weights, m, v = (arrays[i : i + 3] for i in (0, 3, 6, 9))
         early = len(weights) - LATE
         shapes = [(one.shape[0] // WAYS, *one.shape[1:]) for one in m]
-        parts, late_parts = parts_of(m[:early], 1), parts_of(m[early:], PIECES)
+        parts, late_parts = parts_of(m[:early], [FIRST] + [(1,)] * (early - 1)), parts_of(m[early:], [PIECES] * LATE)
 
         def slots(some, number, dtype=jnp.bfloat16):
             return [pltpu.VMEM((*number, *one), dtype) for one in some]

time: 346 us -> 344 us (level)
  no operation moved by 1% of the time
where the time goes in v5:
time: 344 us
  Pallas kernels  344 us (100%)
    pallas_call x1, Pallas kernels, step(): pl.pallas_call(functools.partial(first_kernel, chips, early, parts, late_...  267 us
    pallas_call x1, Pallas kernels, step(): pl.pallas_call(functools.partial(second_kernel, chips, late_parts), out_s...  61.7 us
    pallas_call x2, Pallas kernels, out(): pl.pallas_call(functools.partial(settle, len(arrays)), out_shape=[*shapes...  15.4 us

profile of v5, /device:TPU:21, one launch (start us, length us, event | category | flops | bytes accessed | tf_op | source)
XLA Modules:
  0.0 344.3 jit_solution(5087765903268229422)
XLA Ops:
  0.6 266.5 %shard_map.187 = (bf16[2,1024,2816]{2,1,0:T(8,128)(2,1)S(1)}, bf16[2,1024,2816]{2,1,0:T(8,128)(2,1)S(1)}, f32[2,64,2816]{2,1,0:T(8,128)S(1)}, f32[2,64,2816]{2,1...) custom-call(bf16[1,2,1024,2816]{3,2,1,0:T(8,128)(2,1)} %refs_0_.2, ...), custom_call_target="tpu_custom_call" | custom-call | tf_op jit(solution)/shard_map/pallas_call | solution.py:568
  267.2 9.6 %shard_map.188 = (bf16[2,1024,2816]{2,1,0:T(8,128)(2,1)}, bf16[2,1024,2816]{2,1,0:T(8,128)(2,1)}, f32[2,64,2816]{2,1,0:T(8,128)}, f32[2,64,2816]{2,1,0:T(8,128)}...) custom-call(bf16[2,1024,2816]{2,1,0:T(8,128)(2,1)S(1)} %get-tuple-element.32.refs_0_, ...), custom_call_target="tpu_custom_call" | custom-call | tf_op jit(solution)/shard_map/pallas_call | solution.py:548
  276.8 61.7 %shard_map.189 = (bf16[2,2816,1024]{2,1,0:T(8,128)(2,1)S(1)}, f32[2,176,1024]{2,1,0:T(8,128)S(1)}, f32[2,176,1024]{2,1,0:T(8,128)S(1)}) custom-call(bf16[1,2,2816,1024]{3,2,1,0:T(8,128)(2,1)} %refs_0_.3, bf16[2,2816,1024]{2,1,0:T(8,128)(2,1)} %refs_1_.3, f32[2,176,1024]{2,1,0:T(8,128)} %refs_2_.3, f32[2,176,1024]{2,1,0:T(8,128)} %refs_3_.3, ...), custom_call_target="tpu_custom_call" | custom-call | tf_op jit(solution)/shard_map/pallas_call | solution.py:595
  338.5 5.8 %shard_map.190 = (bf16[2,2816,1024]{2,1,0:T(8,128)(2,1)}, f32[2,176,1024]{2,1,0:T(8,128)}, f32[2,176,1024]{2,1,0:T(8,128)}, f32[8,128]{1,0:T(8,128)}) custom-call(bf16[2,2816,1024]{2,1,0:T(8,128)(2,1)S(1)} %get-tuple-element.45.refs_0_, f32[2,176,1024]{2,1,0:T(8,128)S(1)} %get-tuple-element.46.refs_1_, f32[2,176,1024]{2,1,0:T(8,128)S(1)} %get-tuple-element.47.refs_2_), custom_call_target="tpu_custom_call" | custom-call | tf_op jit(solution)/shard_map/pallas_call | solution.py:548

commit v6 on v5

--- a/solution.py
+++ b/solution.py
@@ -528,7 +528,6 @@
     ]
     for copy in copies:
         copy.start()
-    refs[2 * count][...] = jnp.zeros_like(refs[2 * count])
     for copy in copies:
         copy.wait()
 
@@ -545,15 +544,14 @@
     def out(arrays):
         layers = max(one.shape[0] for one in arrays)
         shapes = [jax.ShapeDtypeStruct(one.shape, one.dtype) for one in arrays]
-        *whole, token = pl.pallas_call(
+        return pl.pallas_call(
             functools.partial(settle, len(arrays)),
-            out_shape=[*shapes, jax.ShapeDtypeStruct((8, 128), jnp.float32)],
+            out_shape=shapes,
             in_specs=[vmem] * len(arrays),
-            out_specs=[any_of] * len(arrays) + [vmem],
+            out_specs=[any_of] * len(arrays),
             scratch_shapes=[dma((len(arrays), layers))],
             compiler_params=pltpu.CompilerParams(vmem_limit_bytes=2 * mib),
         )(*(pltpu.with_memory_space_constraint(one, pltpu.VMEM) for one in arrays))
-        return whole, token
 
     def step(*arrays):
         terms, weights, m, v = (arrays[i : i + 3] for i in (0, 3, 6, 9))
@@ -590,7 +588,7 @@
             compiler_params=pltpu.CompilerParams(collective_id=0, has_side_effects=True, vmem_limit_bytes=24 * mib),
         )(*in_hbm(arrays))
         (w1, m1, v1), rest = (results[i : i + early] for i in (0, early, 2 * early)), results[3 * early :]
-        done, token = out([*w1, *m1, *v1])
+        done = out([*w1, *m1, *v1])
         late = [one for kind in (terms, weights, m, v) for one in kind[early:]]
         results = pl.pallas_call(
             functools.partial(second_kernel, chips, late_parts),
@@ -603,8 +601,8 @@
                 *semaphores(chips, len(late_parts), LATE, KEPT + RING + GATHER),
             ],
             compiler_params=pltpu.CompilerParams(collective_id=1, has_side_effects=True, vmem_limit_bytes=8 * mib),
-        )(*in_hbm([*late, *rest]), token)
-        then, _ = out(results)
+        )(*in_hbm([*late, *rest, done[-1]]))
+        then = out(results)
         return tuple(
             one
             for i in range(3)

time: 344 us -> 344 us (level)
  no operation moved by 1% of the time
where the time goes in v6:
time: 344 us
  Pallas kernels  343 us (100%)
    pallas_call x1, Pallas kernels, step(): pl.pallas_call(functools.partial(first_kernel, chips, early, parts, late_...  267 us
    pallas_call x1, Pallas kernels, step(): pl.pallas_call(functools.partial(second_kernel, chips, late_parts), out_s...  61.7 us
    pallas_call x2, Pallas kernels, out(): pl.pallas_call(functools.partial(settle, len(arrays)), out_shape=shapes,...  14.8 us

profile of v6, /device:TPU:21, one launch (start us, length us, event | category | flops | bytes accessed | tf_op | source)
XLA Modules:
  0.0 343.7 jit_solution(17350644505084176246)
XLA Ops:
  0.6 266.5 %shard_map.187 = (bf16[2,1024,2816]{2,1,0:T(8,128)(2,1)S(1)}, bf16[2,1024,2816]{2,1,0:T(8,128)(2,1)S(1)}, f32[2,64,2816]{2,1,0:T(8,128)S(1)}, f32[2,64,2816]{2,1...) custom-call(bf16[1,2,1024,2816]{3,2,1,0:T(8,128)(2,1)} %refs_0_.2, ...), custom_call_target="tpu_custom_call" | custom-call | tf_op jit(solution)/shard_map/pallas_call | solution.py:566
  267.2 9.6 %shard_map.188 = (bf16[2,1024,2816]{2,1,0:T(8,128)(2,1)}, bf16[2,1024,2816]{2,1,0:T(8,128)(2,1)}, f32[2,64,2816]{2,1,0:T(8,128)}, f32[2,64,2816]{2,1,0:T(8,128)}...) custom-call(bf16[2,1024,2816]{2,1,0:T(8,128)(2,1)S(1)} %get-tuple-element.31.refs_0_, ...), custom_call_target="tpu_custom_call" | custom-call | tf_op jit(solution)/shard_map/pallas_call | solution.py:547
  276.8 61.7 %shard_map.189 = (bf16[2,2816,1024]{2,1,0:T(8,128)(2,1)S(1)}, f32[2,176,1024]{2,1,0:T(8,128)S(1)}, f32[2,176,1024]{2,1,0:T(8,128)S(1)}) custom-call(bf16[1,2,2816,1024]{3,2,1,0:T(8,128)(2,1)} %refs_0_.3, bf16[2,2816,1024]{2,1,0:T(8,128)(2,1)} %refs_1_.3, f32[2,176,1024]{2,1,0:T(8,128)} %refs_2_.3, f32[2,176,1024]{2,1,0:T(8,128)} %refs_3_.3, ...), custom_call_target="tpu_custom_call" | custom-call | tf_op jit(solution)/shard_map/pallas_call | solution.py:593
  338.5 5.2 %shard_map.190 = (bf16[2,2816,1024]{2,1,0:T(8,128)(2,1)}, f32[2,176,1024]{2,1,0:T(8,128)}, f32[2,176,1024]{2,1,0:T(8,128)}) custom-call(bf16[2,2816,1024]{2,1,0:T(8,128)(2,1)S(1)} %get-tuple-element.44.refs_0_, f32[2,176,1024]{2,1,0:T(8,128)S(1)} %get-tuple-element.45.refs_1_, f32[2,176,1024]{2,1,0:T(8,128)S(1)} %get-tuple-element.46.refs_2_), custom_call_target="tpu_custom_call" | custom-call | tf_op jit(solution)/shard_map/pallas_call | solution.py:547

commit v7 on v6

--- a/solution.py
+++ b/solution.py
@@ -13,7 +13,7 @@
 WAYS = 2
 LATE = 1
 FIRST = (1, 3)
-PIECES = (1, 1, 1, 1)
+PIECES = (3, 3, 3, 2)
 
 
 def adamw(w, m, v, g):
@@ -104,7 +104,7 @@
         return pltpu.make_async_remote_copy(
             g[k].at[0, layers(p), where],
             w_out[k].at[layers(p), where],
-            sems.first_send.at[p],
+            sems.give_send.at[k],
             sems.first_recv.at[p],
             device_id=at.partner,
         )
@@ -239,10 +239,12 @@
         gather(t, p).start()
 
     def may_side(p):
-        pl.semaphore_signal(sems.free.at[p], inc=1, device_id=at.partner)
+        if closes[p]:
+            pl.semaphore_signal(sems.free.at[parts[p][0]], inc=1, device_id=at.partner)
 
     def first_side(p):
-        pl.semaphore_wait(sems.free.at[p], 1)
+        if opens[p]:
+            pl.semaphore_wait(sems.free.at[parts[p][0]], 1)
         side(0, p).start()
 
     def onward(t, p, which=None):
@@ -261,9 +263,7 @@
 
     def end_give():
         for k in range(len(w_out)):
-            wait_all(blocks(k, at.last), sems.give_send.at[k])
-        for p in e.parts:
-            give(0, p).wait_send()
+            wait_all(blocks(k, at.chips), sems.give_send.at[k])
 
     for one in (
         fetch, load_own, give, give_all, add, load_state, wait_all, all_of, update, reduce_middle, may_land, gather_after, may_side, first_side, onward, end_gather, end_give,
@@ -273,7 +273,7 @@
     return e
 
 
-GIVE = ("first_send", "first_recv", "give_send", "give_recv")
+GIVE = ("first_recv", "give_send", "give_recv")
 KEPT = ("kept",)
 RING = ("own", "ring_send", "ring_recv", "state")
 GATHER = ("ag_send", "side_send", "side_recv", "free", "clear")
@@ -282,10 +282,10 @@
 def semaphores(chips, count, weights, names):
     dma, plain = pltpu.SemaphoreType.DMA, pltpu.SemaphoreType.REGULAR
     shape = dict(
-        first_send=dma((count,)), first_recv=dma((count,)), give_send=dma((weights,)), give_recv=dma((chips, weights)),
+        first_recv=dma((count,)), give_send=dma((weights,)), give_recv=dma((chips, weights)),
         kept=dma((2, weights)), own=dma((2, weights)), ring_send=dma((2, count)), ring_recv=dma((chips - 1, count)),
         state=dma((3, weights)), ag_send=dma((weights,)), side_send=dma((weights,)),
-        side_recv=dma((weights,)), free=plain((count,)), clear=plain((2, count)),
+        side_recv=dma((weights,)), free=plain((weights,)), clear=plain((2, count)),
     )
     return [shape[name] for name in names]
 
@@ -371,9 +371,8 @@
         a.update(p)
         a.gather_after(0, 0, p)
         a.may_side(p)
-        if p:
-            a.first_side(p - 1)
-    a.first_side(len(parts) - 1)
+    for p in a.parts:
+        a.first_side(p)
     for p in a.parts:
         a.ring(last - 1, p).wait_send()
         a.may_land(1, p)

time: 344 us -> 344 us (level)
  no operation moved by 1% of the time
where the time goes in v7:
time: 344 us
  Pallas kernels  343 us (100%)
    pallas_call x1, Pallas kernels, step(): pl.pallas_call(functools.partial(first_kernel, chips, early, parts, late_...  266 us
    pallas_call x1, Pallas kernels, step(): pl.pallas_call(functools.partial(second_kernel, chips, late_parts), out_s...  61.8 us
    pallas_call x2, Pallas kernels, out(): pl.pallas_call(functools.partial(settle, len(arrays)), out_shape=shapes,...  14.8 us

profile of v7, /device:TPU:21, one launch (start us, length us, event | category | flops | bytes accessed | tf_op | source)
XLA Modules:
  0.0 343.6 jit_solution(9179233222600927530)
XLA Ops:
  0.6 266.3 %shard_map.187 = (bf16[2,1024,2816]{2,1,0:T(8,128)(2,1)S(1)}, bf16[2,1024,2816]{2,1,0:T(8,128)(2,1)S(1)}, f32[2,64,2816]{2,1,0:T(8,128)S(1)}, f32[2,64,2816]{2,1...) custom-call(bf16[1,2,1024,2816]{3,2,1,0:T(8,128)(2,1)} %refs_0_.2, ...), custom_call_target="tpu_custom_call" | custom-call | tf_op jit(solution)/shard_map/pallas_call | solution.py:565
  267.0 9.6 %shard_map.188 = (bf16[2,1024,2816]{2,1,0:T(8,128)(2,1)}, bf16[2,1024,2816]{2,1,0:T(8,128)(2,1)}, f32[2,64,2816]{2,1,0:T(8,128)}, f32[2,64,2816]{2,1,0:T(8,128)}...) custom-call(bf16[2,1024,2816]{2,1,0:T(8,128)(2,1)S(1)} %get-tuple-element.31.refs_0_, ...), custom_call_target="tpu_custom_call" | custom-call | tf_op jit(solution)/shard_map/pallas_call | solution.py:546
  276.6 61.8 %shard_map.189 = (bf16[2,2816,1024]{2,1,0:T(8,128)(2,1)S(1)}, f32[2,176,1024]{2,1,0:T(8,128)S(1)}, f32[2,176,1024]{2,1,0:T(8,128)S(1)}) custom-call(bf16[1,2,2816,1024]{3,2,1,0:T(8,128)(2,1)} %refs_0_.3, bf16[2,2816,1024]{2,1,0:T(8,128)(2,1)} %refs_1_.3, f32[2,176,1024]{2,1,0:T(8,128)} %refs_2_.3, f32[2,176,1024]{2,1,0:T(8,128)} %refs_3_.3, ...), custom_call_target="tpu_custom_call" | custom-call | tf_op jit(solution)/shard_map/pallas_call | solution.py:592
  338.4 5.2 %shard_map.190 = (bf16[2,2816,1024]{2,1,0:T(8,128)(2,1)}, f32[2,176,1024]{2,1,0:T(8,128)}, f32[2,176,1024]{2,1,0:T(8,128)}) custom-call(bf16[2,2816,1024]{2,1,0:T(8,128)(2,1)S(1)} %get-tuple-element.44.refs_0_, f32[2,176,1024]{2,1,0:T(8,128)S(1)} %get-tuple-element.45.refs_1_, f32[2,176,1024]{2,1,0:T(8,128)S(1)} %get-tuple-element.46.refs_2_), custom_call_target="tpu_custom_call" | custom-call | tf_op jit(solution)/shard_map/pallas_call | solution.py:546
